TPU v7x, 128 devices: a whole 4x4x4 slice. The times are simulated.
128 devices in a mesh: lon: 8 (over z, y_hi), lat: 16 (over y_lo, x, core).
Axes of the slice: x: 4, y: 4 (y_hi: 2, y_lo: 2; y = y_hi * 2 + y_lo), z: 4, core: 2. Of those that a mesh axis runs over, the one named last changes fastest.
Arguments:
- fields: float32 [4, 8, 1024, 3600], P(None, None, 'lat', 'lon'), may hold values from -6 to 6
- thickness: float32 [8], replicated, may hold values from 5 to 250
- cutoff: int32 [256], replicated, may hold values from 2 to 1800
- barotropic: float32 [3, 1024, 3600], P(None, 'lat', 'lon'), may hold values from -6 to 6
- land_sea: int32 [1024, 3600], P('lat', 'lon'), may hold values 0 or 1
Outputs:
- filtered_tracers: float32 [2, 8, 1024, 3600], P(None, None, 'lat', 'lon')
- velocity: float32 [2, 8, 1024, 3600], P(None, None, 'lat', 'lon')
- sea_level: float32 [1024, 3600], P('lat', 'lon')
Inputs may be any that keep to these rules, and one draw needn't show every extreme that they name: `cutoff`: each filtered row's highest kept wavenumber.
All inputs are finite; a program needn't handle non-finite values. No bound on the sum of `land_sea` on one device may be relied on, other than what follows from the above.
Results may differ from a plain program's by a relative error of at most 0.0003.
Values sent between devices are 32-bit elements; how exact they have to be, the bound alone decides.
A program may use at most 128 MiB of HBM per device.

v0:
```python
import math

import jax
import jax.numpy as jnp
from jax import lax
from jax.sharding import PartitionSpec as P

POLE_DEV = 2
SUB = 20


wave_coef = 0.65
highest = lax.Precision.HIGHEST


def with_halo(value, sides, width):
    for axis, dim in sides:
        devices, length = (lax.axis_size(axis), value.shape[dim])
        up = [(i, (i + 1) % devices) for i in range(devices)]
        down = [(j, i) for i, j in up]
        last = lax.slice_in_dim(value, length - width, length, axis=dim)
        initial = lax.slice_in_dim(value, 0, width, axis=dim)
        before = lax.ppermute(last, axis, up)
        after = lax.ppermute(initial, axis, down)
        value = jnp.concatenate([before, value, after], axis=dim)
    return value


def trig_tables(rows_len, cols_len, period):
    product = lax.broadcasted_iota(jnp.int32, (rows_len, cols_len), 0) * lax.broadcasted_iota(
        jnp.int32, (rows_len, cols_len), 1
    )
    angles = (product % period).astype(jnp.float32) * (2.0 * math.pi / period)
    return (jnp.cos(angles), jnp.sin(angles))


def spectral_cut(values, row_cuts):
    item_count, circle_len = values.shape
    first_len = max((d for d in range(1, math.isqrt(circle_len) + 1) if circle_len % d == 0))
    second_len = circle_len // first_len
    cos_first, sin_first = trig_tables(first_len, first_len, first_len)
    cos_second, sin_second = trig_tables(second_len, second_len, second_len)
    twist_cos, twist_sin = trig_tables(first_len, second_len, circle_len)
    grid = values.reshape(item_count, first_len, second_len)
    step_real = jnp.einsum("inb,nm->imb", grid, cos_first, precision=highest)
    step_imag = -jnp.einsum("inb,nm->imb", grid, sin_first, precision=highest)
    turn_real = step_real * twist_cos + step_imag * twist_sin
    turn_imag = step_imag * twist_cos - step_real * twist_sin
    spec_real = jnp.einsum("imb,bk->imk", turn_real, cos_second, precision=highest) + jnp.einsum(
        "imb,bk->imk", turn_imag, sin_second, precision=highest
    )
    spec_imag = jnp.einsum("imb,bk->imk", turn_imag, cos_second, precision=highest) - jnp.einsum(
        "imb,bk->imk", turn_real, sin_second, precision=highest
    )
    wavenumber = lax.broadcasted_iota(
        jnp.int32, (first_len, second_len), 0
    ) + first_len * lax.broadcasted_iota(jnp.int32, (first_len, second_len), 1)
    folded = jnp.minimum(wavenumber, circle_len - wavenumber)
    kept_mask = jnp.where(folded[None, :, :] <= row_cuts[:, None, None], 1.0 / circle_len, 0.0)
    spec_real = spec_real * kept_mask
    spec_imag = spec_imag * kept_mask
    part_real = jnp.einsum("imq,qk->imk", spec_real, cos_second, precision=highest) - jnp.einsum(
        "imq,qk->imk", spec_imag, sin_second, precision=highest
    )
    part_imag = jnp.einsum("imq,qk->imk", spec_real, sin_second, precision=highest) + jnp.einsum(
        "imq,qk->imk", spec_imag, cos_second, precision=highest
    )
    back_real = part_real * twist_cos - part_imag * twist_sin
    back_imag = part_real * twist_sin + part_imag * twist_cos
    rebuilt = jnp.einsum("imk,mj->ijk", back_real, cos_first, precision=highest) - jnp.einsum(
        "imk,mj->ijk", back_imag, sin_first, precision=highest
    )
    return rebuilt.reshape(item_count, circle_len)


def row_cutoffs(cutoff, band, item_ids, band_rows, total_rows):
    pole_rows = cutoff.shape[0] // 2
    global_row = band * band_rows + item_ids % band_rows
    table_index = jnp.where(
        global_row < pole_rows, global_row, global_row - (total_rows - 2 * pole_rows)
    )
    matches = table_index[:, None] == lax.broadcasted_iota(jnp.int32, (1, 2 * pole_rows), 1)
    return jnp.sum(jnp.where(matches, cutoff[None, :], 0), axis=1)


def body(fields, thickness, cutoff, barotropic, land_sea):
    lon_count = lax.axis_size("lon")
    lat_count = lax.axis_size("lat")
    lat_index = lax.axis_index("lat")
    lon_index = lax.axis_index("lon")
    components, levels, band_rows, tile_cols = fields.shape
    total_rows = band_rows * lat_count
    total_items = components * levels * band_rows
    share_items = total_items // lon_count
    flattened = fields.reshape(total_items, tile_cols)
    circled = lax.all_to_all(flattened, "lon", split_axis=0, concat_axis=1, tiled=True)
    item_ids = lon_index * share_items + lax.iota(jnp.int32, share_items)
    north_pole = lat_index < POLE_DEV
    south_pole = lat_index >= lat_count - POLE_DEV
    row_cuts = row_cutoffs(cutoff, lat_index, item_ids, band_rows, total_rows)
    result = lax.cond(
        north_pole | south_pole,
        lambda values: spectral_cut(values, row_cuts),
        lambda values: values,
        circled,
    )
    returned = lax.all_to_all(result, "lon", split_axis=1, concat_axis=0, tiled=True)
    filtered = returned.reshape(components, levels, band_rows, tile_cols)
    rim_width = 4
    mask_wide = with_halo(land_sea, (("lon", 1), ("lat", 0)), rim_width + 1)
    ocean_wide = mask_wide.astype(jnp.float32)
    pad_rows = (
        lat_index * band_rows - rim_width - 1 + lax.iota(jnp.int32, band_rows + 2 * rim_width + 2)
    ) % total_rows
    east_wide = ocean_wide * jnp.roll(ocean_wide, -1, 1)
    north_wide = (
        ocean_wide
        * jnp.roll(ocean_wide, -1, 0)
        * (pad_rows != total_rows - 1).astype(jnp.float32)[:, None]
    )
    ocean_pad = ocean_wide[1:-1, 1:-1]
    east_pad = east_wide[1:-1, 1:-1]
    north_pad = north_wide[1:-1, 1:-1]

    def advance(cycle_index, state_now):
        padded = with_halo(state_now, (("lon", 2), ("lat", 1)), rim_width)
        surface = padded[0]
        eastward = padded[1] * east_pad
        northward = padded[2] * north_pad
        for subcycle in range(rim_width):
            divergence = eastward - jnp.roll(eastward, 1, 1) + northward - jnp.roll(northward, 1, 0)
            surface = surface - wave_coef * ocean_pad * divergence
            eastward = east_pad * (eastward - wave_coef * (jnp.roll(surface, -1, 1) - surface))
            northward = north_pad * (northward - wave_coef * (jnp.roll(surface, -1, 0) - surface))
        return jnp.stack([surface, eastward, northward])[
            :, rim_width:-rim_width, rim_width:-rim_width
        ]

    final_state = lax.fori_loop(0, SUB // rim_width, advance, barotropic)
    east_mid = east_pad[rim_width:-rim_width, rim_width:-rim_width]
    north_mid = north_pad[rim_width:-rim_width, rim_width:-rim_width]
    weights = thickness / jnp.sum(thickness)
    currents = filtered[2:]
    column = jnp.einsum("k,ckij->cij", weights, currents, precision=highest)
    velocity = jnp.stack([east_mid, north_mid])[:, None] * (
        currents - column[:, None] + final_state[1:][:, None]
    )
    return (filtered[:2], velocity, final_state[0])


def solution(mesh):
    return jax.shard_map(
        body,
        mesh=mesh,
        in_specs=(P(None, None, "lat", "lon"), P(), P(), P(None, "lat", "lon"), P("lat", "lon")),
        out_specs=(P(None, None, "lat", "lon"), P(None, None, "lat", "lon"), P("lat", "lon")),
        check_vma=False,
    )
```

profile of v0, /device:TPU:0, one launch (start us, length us, event | category | flops | bytes accessed | tf_op | source)
XLA Modules:
  0.0 315.3 jit_solution(11312199765640784743)
XLA Ops:
  0.6 5.3 %copy.115 = f32[8,256,450]{1,2,0:T(8,128)} copy(f32[8,256,450]{2,1,0:T(8,128)} %bitcast.272) | data formatting | bytes 7372800 | tf_op jit(solution)/shard_map/all_to_all | solution.py:96
  5.9 8.2 %all-to-all-start = ((f32[8,256,450]{1,2,0:T(8,128)}), f32[8,256,450]{1,2,0:T(8,128)}, u32[]{:S(2)}, u32[]{:S(2)}) async-start(f32[8,256,450]{1,2,0:T(8,128)} %copy.115), calls=%async_computation | async-start | bytes 7471104 | tf_op jit(solution)/shard_map/all_to_all | solution.py:96
  14.2 3.5 %collective-permute-start.4 = (s32[64,5]{1,0:T(8,128)S(1)}, s32[64,5]{1,0:T(8,128)S(1)}, u32[]{:S(2)}, u32[]{:S(2)}) collective-permute-start(s32[64,5]{1,0:T(8,128)S(1)} %get-tuple-element.334), channel_id=1, source_target_pairs={{0,16},{16,32},{32,48},{48,64},{64,80},{80,96},{96,112},{112,0},{1... | collective-permute-start | bytes 3848 | tf_op jit(solution)/shard_map/ppermute | solution.py:23
  17.7 2.2 collective-permute-start.5
  19.9 41.3 %collective-permute-done.4 = s32[64,5]{1,0:T(8,128)S(1)} collective-permute-done((s32[64,5]{1,0:T(8,128)S(1)}, s32[64,5]{1,0:T(8,128)S(1)}, u32[]{:S(2)}, u32[]{:S(2)}) %collective-permute-start.4) | collective-permute-done | bytes 1312 | tf_op jit(solution)/shard_map/ppermute | solution.py:23
  61.3 3.8 %collective-permute-start.7 = (s32[5,460]{1,0:T(8,128)S(1)}, s32[5,460]{1,0:T(8,128)S(1)}, u32[]{:S(2)}, u32[]{:S(2)}) collective-permute-start(s32[5,460]{1,0:T(8,128)S(1)} %get-tuple-element.331), channel_id=1, source_target_pairs={{1,0},{2,1},{3,2},{4,3},{5,4},{6,5},{7,6},{8,7},{9,8},{10,9},{11,1... | collective-permute-start | bytes 27608 | tf_op jit(solution)/shard_map/ppermute | solution.py:24
  67.4 3.6 %all_to_all.32 = f32[256,3600]{0,1:T(8,128)} reshape(f32[256,8,450]{0,2,1:T(8,128)} %bitcast.39) | data formatting | bytes 7372800 | tf_op jit(solution)/shard_map/all_to_all | solution.py:96
  71.0 88.4 %conditional.1 = (f32[256,3600]{0,1:T(8,128)}) conditional(s32[]{:T(128)} %convert_element_type.71, f32[256,3600]{0,1:T(8,128)} %all_to_all.32, (f32[256,3600]{0,1:T(8,128)}, s32[]{:T(128)}, s32[]{:T(128)}, s32[256,1]{0,1:T(1,128)S(1)}, s32[]{:T(128)}, /*index=5*/s32[256,256]{1,0:T(8,128)S(1)}, s32[256]{0:T(256)S(1)}) %tuple.175), branch_computations={%region_0.1_spmd, %region_1.3_spmd.clone.clone} | conditional | flops 7985373696 | bytes 159001056 | solution.py:101
  71.8 4.9 %reshape.244 = f32[256,60,60]{0,2,1:T(8,128)} reshape(f32[256,3600]{0,1:T(8,128)} %get-tuple-element.223) | data formatting | bytes 7372800 | tf_op jit(solution)/shard_map/cond/branch_1_fun/reshape | solution.py:44
  76.7 8.0 %fusion.86 = f32[60,256,60]{1,0,2:T(8,128)S(1)} fusion(f32[256,60,60]{0,2,1:T(8,128)} %reshape.244), kind=kOutput, calls=%fused_computation.157 | convolution fusion | flops 663584384 | bytes 7372800 | tf_op jit(solution)/shard_map/cond/branch_1_fun/inb,nm->imb/dot_general | solution.py:46
  84.8 7.8 %add_bitcast_fusion = (f32[256,60,60]{0,1,2:T(8,128)S(1)}, f32[256,60,60]{0,1,2:T(8,128)S(1)}) fusion(f32[60,256,60]{1,0,2:T(8,128)S(1)} %fusion.86, f32[60,60]{0,1:T(8,128)S(1)} %get-tuple-element.258, f32[60,60]{0,1:T(8,128)S(1)} %get-tuple-element.259, f32[256,60,60]{0,2,1:T(8,128)S(1)} %copy-done.1), kind=kOutput, calls=%fused_computation.148 | convolution fusion | flops 670035584 | bytes 14774400 | tf_op jit(solution)/shard_map/cond/branch_1_fun/inb,nm->imb/dot_general | solution.py:45
  92.5 6.2 %fusion.78 = f32[256,60,60]{0,2,1:T(8,128)S(1)} fusion(f32[256,60,60]{0,1,2:T(8,128)S(1)} %get-tuple-element.257), kind=kOutput, calls=%fused_computation.149 | convolution fusion | flops 663584384 | bytes 7372800 | tf_op jit(solution)/shard_map/cond/branch_1_fun/imb,bk->imk/dot_general | solution.py:52
  98.8 7.7 %select_multiply_fusion = f32[256,60,60]{0,2,1:T(8,128)S(1)} fusion(f32[256,60,60]{0,2,1:T(8,128)S(1)} %fusion.78, f32[256,60,60]{0,1,2:T(8,128)S(1)} %get-tuple-element.256, s32[256]{0:T(256)S(1)} %select_reduce_fusion, s32[60,60]{1,0:T(8,128)S(1)} %copy.124), kind=kOutput, calls=%fused_computation.138 | convolution fusion | flops 667270784 | bytes 11074624 | tf_op jit(solution)/shard_map/cond/branch_1_fun/imb,bk->imk/dot_general | solution.py:52
  106.5 6.2 %fusion.80 = f32[256,60,60]{0,2,1:T(8,128)S(1)} fusion(f32[256,60,60]{0,1,2:T(8,128)S(1)} %get-tuple-element.257), kind=kOutput, calls=%fused_computation.151 | convolution fusion | flops 663584384 | bytes 7372800 | tf_op jit(solution)/shard_map/cond/branch_1_fun/imb,bk->imk/dot_general | solution.py:49
  112.7 7.4 %select_multiply_fusion.1 = f32[256,60,60]{0,2,1:T(8,128)S(1)} fusion(f32[256,60,60]{0,2,1:T(8,128)S(1)} %fusion.80, f32[256,60,60]{0,1,2:T(8,128)S(1)} %get-tuple-element.256, s32[256]{0:T(256)S(1)} %select_reduce_fusion, s32[60,60]{1,0:T(8,128)S(1)} %copy.124), kind=kOutput, calls=%fused_computation.139 | convolution fusion | flops 667270784 | bytes 11074624 | tf_op jit(solution)/shard_map/cond/branch_1_fun/imb,bk->imk/dot_general | solution.py:49
  120.1 3.9 %fusion.101 = f32[256,60,60]{0,2,1:T(8,128)S(1)} fusion(f32[256,60,60]{0,2,1:T(8,128)S(1)} %select_multiply_fusion.1), kind=kOutput, calls=%fused_computation.172 | convolution fusion | flops 663584384 | bytes 7372800 | tf_op jit(solution)/shard_map/cond/branch_1_fun/imq,qk->imk/dot_general | solution.py:65
  124.1 3.9 %fusion.110 = f32[256,60,60]{0,2,1:T(8,128)S(1)} fusion(f32[256,60,60]{0,2,1:T(8,128)S(1)} %select_multiply_fusion.1), kind=kOutput, calls=%fused_computation.181 | convolution fusion | flops 663584384 | bytes 7372800 | tf_op jit(solution)/shard_map/cond/branch_1_fun/imq,qk->imk/dot_general | solution.py:62
  128.0 4.2 %convolution_subtract_fusion = f32[256,60,60]{0,2,1:T(8,128)S(1)} fusion(f32[256,60,60]{0,2,1:T(8,128)S(1)} %fusion.110, f32[256,60,60]{0,2,1:T(8,128)S(1)} %select_multiply_fusion), kind=kOutput, calls=%fused_computation.162 | convolution fusion | flops 664505984 | bytes 11059200 | tf_op jit(solution)/shard_map/cond/branch_1_fun/imq,qk->imk/dot_general | solution.py:62
  132.2 6.1 %multiply_subtract_fusion = (f32[256,60,60]{0,2,1:T(8,128)S(1)}, f32[256,60,60]{0,2,1:T(8,128)S(1)}) fusion(f32[256,60,60]{0,2,1:T(8,128)S(1)} %convolution_subtract_fusion, f32[60,60]{1,0:T(8,128)S(1)} %copy.126, f32[60,60]{1,0:T(8,128)S(1)} %copy.125, f32[256,60,60]{0,2,1:T(8,128)S(1)} %fusion.101, f32[256,60,60]{0,2,1:T(8,128)S(1)} %select_multiply_fusion), kind=kOutput, calls=%fused_computation.146 | convolution fusion | flops 670035584 | bytes 18460800 | tf_op jit(solution)/shard_map/cond/branch_1_fun/imq,qk->imk/dot_general | solution.py:65
  138.3 5.8 %fusion.74 = f32[60,256,60]{1,0,2:T(8,128)S(1)} fusion(f32[256,60,60]{0,2,1:T(8,128)S(1)} %get-tuple-element.255), kind=kOutput, calls=%fused_computation.140 | convolution fusion | flops 663584384 | bytes 7372800 | tf_op jit(solution)/shard_map/cond/branch_1_fun/imk,mj->ijk/dot_general | solution.py:70
  144.1 6.3 %subtract_bitcast_fusion = f32[256,60,60]{0,1,2:T(8,128)S(1)} fusion(f32[60,256,60]{1,0,2:T(8,128)S(1)} %fusion.74, f32[256,60,60]{0,2,1:T(8,128)S(1)} %get-tuple-element.254), kind=kOutput, calls=%fused_computation.144 | convolution fusion | flops 664505984 | bytes 11059200 | tf_op jit(solution)/shard_map/cond/branch_1_fun/imk,mj->ijk/dot_general | solution.py:70
  150.4 4.0 %copy.129 = f32[256,60,60]{0,2,1:T(8,128)} copy(f32[256,60,60]{0,1,2:T(8,128)S(1)} %subtract_bitcast_fusion) | data formatting | bytes 7372800 | tf_op jit(solution)/shard_map/cond/branch_1_fun/sub | solution.py:70
  154.4 4.8 %reshape.245 = f32[256,3600]{0,1:T(8,128)} reshape(f32[256,60,60]{0,2,1:T(8,128)} %copy.129) | data formatting | bytes 7372800 | tf_op jit(solution)/shard_map/cond/branch_1_fun/reshape | solution.py:73
  159.4 3.6 %all_to_all.33 = f32[256,8,450]{0,2,1:T(8,128)} reshape(f32[256,3600]{0,1:T(8,128)} %get-tuple-element.537) | data formatting | bytes 7372800 | tf_op jit(solution)/shard_map/all_to_all | solution.py:107
  162.9 4.6 %all-to-all-start.1 = ((f32[256,8,450]{0,2,1:T(8,128)}), f32[256,8,450]{0,2,1:T(8,128)}, u32[]{:S(2)}, u32[]{:S(2)}) async-start(f32[256,8,450]{0,2,1:T(8,128)} %all_to_all.33), calls=%async_computation.1 | async-start | bytes 7471104 | tf_op jit(solution)/shard_map/all_to_all | solution.py:107
  167.6 132.5 %while.10 = (s32[]{:T(128)}, f32[3,64,450]{2,1,0:T(8,128)S(1)}, f32[72,458]{1,0:T(8,128)S(1)}, f32[72,458]{1,0:T(8,128)S(1)}, f32[72,458]{1,0:T(8,128)S(1)}, /*index=5*/s32[]{:T(128)}) while((s32[]{:T(128)}, f32[3,64,450]{2,1,0:T(8,128)S(1)}, f32[72,458]{1,0:T(8,128)S(1)}, f32[72,458]{1,0:T(8,128)S(1)}, f32[72,458]{1,0:T(8,128)S(1)}, ...), condition=%wide.region_5.6_spmd, body=%wide.region_4.5_spmd.sunk | while | flops 5437970 | bytes 21927012 | solution.py:139
  167.7 5.6 %collective-permute-start = (f32[3,64,4]{2,1,0:T(8,128)S(1)}, f32[3,64,4]{2,1,0:T(8,128)S(1)}, u32[]{:S(2)}, u32[]{:S(2)}) collective-permute-start(f32[3,64,4]{2,1,0:T(8,128)S(1)} %get-tuple-element.444), channel_id=1, source_target_pairs={{16,0},{32,16},{48,32},{64,48},{80,64},{96,80},{112,96},{0,112},{1... | collective-permute-start | bytes 9224 | tf_op jit(solution)/shard_map/while/body/eval_jaxpr/ppermute | solution.py:24
  173.3 42.6 %collective-permute-done = f32[3,64,4]{2,1,0:T(8,128)S(1)} collective-permute-done((f32[3,64,4]{2,1,0:T(8,128)S(1)}, f32[3,64,4]{2,1,0:T(8,128)S(1)}, u32[]{:S(2)}, u32[]{:S(2)}) %collective-permute-start) | collective-permute-done | bytes 3104 | tf_op jit(solution)/shard_map/while/body/eval_jaxpr/ppermute | solution.py:24
  221.0 3.8 %collective-permute-done.3 = f32[3,4,458]{2,1,0:T(4,128)S(1)} collective-permute-done((f32[3,4,458]{2,1,0:T(4,128)S(1)}, f32[3,4,458]{2,1,0:T(4,128)S(1)}, u32[]{:S(2)}, u32[]{:S(2)}) %collective-permute-start.3) | collective-permute-done | bytes 22016 | tf_op jit(solution)/shard_map/while/body/eval_jaxpr/ppermute | solution.py:23
  229.6 2.3 collective-permute-start.1
  231.9 2.6 collective-permute-done
  234.5 3.4 %collective-permute-done.1 = f32[3,64,4]{2,1,0:T(8,128)S(1)} collective-permute-done((f32[3,64,4]{2,1,0:T(8,128)S(1)}, f32[3,64,4]{2,1,0:T(8,128)S(1)}, u32[]{:S(2)}, u32[]{:S(2)}) %collective-permute-start.1) | collective-permute-done | bytes 3104 | tf_op jit(solution)/shard_map/while/body/eval_jaxpr/ppermute | solution.py:23
  239.6 3.9 %collective-permute-done.3 = f32[3,4,458]{2,1,0:T(4,128)S(1)} collective-permute-done((f32[3,4,458]{2,1,0:T(4,128)S(1)}, f32[3,4,458]{2,1,0:T(4,128)S(1)}, u32[]{:S(2)}, u32[]{:S(2)}) %collective-permute-start.3) | collective-permute-done | bytes 22016 | tf_op jit(solution)/shard_map/while/body/eval_jaxpr/ppermute | solution.py:23
  248.0 2.5 collective-permute-start.1
  250.5 2.6 collective-permute-done
  253.1 3.2 %collective-permute-done.1 = f32[3,64,4]{2,1,0:T(8,128)S(1)} collective-permute-done((f32[3,64,4]{2,1,0:T(8,128)S(1)}, f32[3,64,4]{2,1,0:T(8,128)S(1)}, u32[]{:S(2)}, u32[]{:S(2)}) %collective-permute-start.1) | collective-permute-done | bytes 3104 | tf_op jit(solution)/shard_map/while/body/eval_jaxpr/ppermute | solution.py:23
  258.0 3.9 %collective-permute-done.3 = f32[3,4,458]{2,1,0:T(4,128)S(1)} collective-permute-done((f32[3,4,458]{2,1,0:T(4,128)S(1)}, f32[3,4,458]{2,1,0:T(4,128)S(1)}, u32[]{:S(2)}, u32[]{:S(2)}) %collective-permute-start.3) | collective-permute-done | bytes 22016 | tf_op jit(solution)/shard_map/while/body/eval_jaxpr/ppermute | solution.py:23
  265.4 3.5 %collective-permute-start.1 = (f32[3,64,4]{2,1,0:T(8,128)S(1)}, f32[3,64,4]{2,1,0:T(8,128)S(1)}, u32[]{:S(2)}, u32[]{:S(2)}) collective-permute-start(f32[3,64,4]{2,1,0:T(8,128)S(1)} %get-tuple-element.445), channel_id=1, source_target_pairs={{0,16},{16,32},{32,48},{48,64},{64,80},{80,96},{96,112},{112,0},{1... | collective-permute-start | bytes 9224 | tf_op jit(solution)/shard_map/while/body/eval_jaxpr/ppermute | solution.py:23
  268.9 2.6 collective-permute-done
  271.5 2.2 collective-permute-done.1
  275.4 3.9 %collective-permute-done.3 = f32[3,4,458]{2,1,0:T(4,128)S(1)} collective-permute-done((f32[3,4,458]{2,1,0:T(4,128)S(1)}, f32[3,4,458]{2,1,0:T(4,128)S(1)}, u32[]{:S(2)}, u32[]{:S(2)}) %collective-permute-start.3) | collective-permute-done | bytes 22016 | tf_op jit(solution)/shard_map/while/body/eval_jaxpr/ppermute | solution.py:23
  282.8 3.5 %collective-permute-start.1 = (f32[3,64,4]{2,1,0:T(8,128)S(1)}, f32[3,64,4]{2,1,0:T(8,128)S(1)}, u32[]{:S(2)}, u32[]{:S(2)}) collective-permute-start(f32[3,64,4]{2,1,0:T(8,128)S(1)} %get-tuple-element.445), channel_id=1, source_target_pairs={{0,16},{16,32},{32,48},{48,64},{64,80},{80,96},{96,112},{112,0},{1... | collective-permute-start | bytes 9224 | tf_op jit(solution)/shard_map/while/body/eval_jaxpr/ppermute | solution.py:23
  286.3 2.6 collective-permute-done
  288.9 2.2 collective-permute-done.1
  292.8 3.9 %collective-permute-done.3 = f32[3,4,458]{2,1,0:T(4,128)S(1)} collective-permute-done((f32[3,4,458]{2,1,0:T(4,128)S(1)}, f32[3,4,458]{2,1,0:T(4,128)S(1)}, u32[]{:S(2)}, u32[]{:S(2)}) %collective-permute-start.3) | collective-permute-done | bytes 22016 | tf_op jit(solution)/shard_map/while/body/eval_jaxpr/ppermute | solution.py:23
  300.9 4.2 %fusion.225 = (f32[4,256,450]{1,2,0:T(8,128)}, f32[4,256,450]{1,2,0:T(8,128)}) fusion(f32[8,256,450]{1,2,0:T(8,128)} %bitcast.40), kind=kLoop, calls=%fused_computation.289 | loop fusion | bytes 7372800 | tf_op jit(solution)/shard_map/slice | solution.py:143
  307.0 3.4 %fusion.212 = f32[1,2,64,450]{3,0,2,1:T(1,128)S(1)} fusion(f32[2,8,64,450]{3,2,1,0:T(8,128)S(1)} %bitcast.270, f32[8]{0:T(128)S(1)} %copy-done.4, f32[]{:T(128)} %reduce_sum.23), kind=kOutput, calls=%fused_computation.265 | convolution fusion | flops 5529608 | bytes 2073636 | tf_op jit(solution)/shard_map/k,ckij->cij/dot_general | solution.py:144
  310.4 2.8 copy.116
  (302 shorter events, 37.7 us)
Async XLA Ops:
  5.9 8.2 %copy-start.2 = (s32[64,450]{1,0:T(8,128)S(1)}, s32[64,450]{1,0:T(8,128)}, u32[]{:S(2)}) copy-start(s32[64,450]{1,0:T(8,128)} %param.13) | copy-start | bytes 345604
  5.9 59.3 %copy-start.4 = (f32[8]{0:T(128)S(1)}, f32[8]{0:T(128)}, u32[]{:S(2)}) copy-start(f32[8]{0:T(128)} %param.10) | copy-start | bytes 100
  5.9 61.4 %all-to-all-start = ((f32[8,256,450]{1,2,0:T(8,128)}), f32[8,256,450]{1,2,0:T(8,128)}, u32[]{:S(2)}, u32[]{:S(2)}) async-start(f32[8,256,450]{1,2,0:T(8,128)} %copy.115), calls=%async_computation | async-start | bytes 7471104 | tf_op jit(solution)/shard_map/all_to_all | solution.py:96
  14.2 47.0 %collective-permute-start.4 = (s32[64,5]{1,0:T(8,128)S(1)}, s32[64,5]{1,0:T(8,128)S(1)}, u32[]{:S(2)}, u32[]{:S(2)}) collective-permute-start(s32[64,5]{1,0:T(8,128)S(1)} %get-tuple-element.334), channel_id=1, source_target_pairs={{0,16},{16,32},{32,48},{48,64},{64,80},{80,96},{96,112},{112,0},{1... | collective-permute-start | bytes 3848 | tf_op jit(solution)/shard_map/ppermute | solution.py:23
  17.7 43.5 %collective-permute-start.5 = (s32[64,5]{1,0:T(8,128)S(1)}, s32[64,5]{1,0:T(8,128)S(1)}, u32[]{:S(2)}, u32[]{:S(2)}) collective-permute-start(s32[64,5]{1,0:T(8,128)S(1)} %get-tuple-element.335), channel_id=1, source_target_pairs={{16,0},{32,16},{48,32},{64,48},{80,64},{96,80},{112,96},{0,112},{1... | collective-permute-start | bytes 3848 | tf_op jit(solution)/shard_map/ppermute | solution.py:24
  61.3 5.3 %collective-permute-start.6 = (s32[5,460]{1,0:T(8,128)S(1)}, s32[5,460]{1,0:T(8,128)S(1)}, u32[]{:S(2)}, u32[]{:S(2)}) collective-permute-start(s32[5,460]{1,0:T(8,128)S(1)} %get-tuple-element.330), channel_id=1, source_target_pairs={{0,1},{1,2},{2,3},{3,4},{4,5},{5,6},{6,7},{7,8},{8,9},{9,10},{10,1... | collective-permute-start | bytes 27608 | tf_op jit(solution)/shard_map/ppermute | solution.py:23
  61.3 5.3 %collective-permute-start.7 = (s32[5,460]{1,0:T(8,128)S(1)}, s32[5,460]{1,0:T(8,128)S(1)}, u32[]{:S(2)}, u32[]{:S(2)}) collective-permute-start(s32[5,460]{1,0:T(8,128)S(1)} %get-tuple-element.331), channel_id=1, source_target_pairs={{1,0},{2,1},{3,2},{4,3},{5,4},{6,5},{7,6},{8,7},{9,8},{10,9},{11,1... | collective-permute-start | bytes 27608 | tf_op jit(solution)/shard_map/ppermute | solution.py:24
  67.3 3.7 %copy-start.3 = (s32[256]{0:T(256)S(1)}, s32[256]{0:T(256)}, u32[]{:S(2)}) copy-start(s32[256]{0:T(256)} %param.11) | copy-start | bytes 3076
  76.7 8.1 %copy-start.1 = (f32[256,60,60]{0,2,1:T(8,128)S(1)}, f32[256,60,60]{0,2,1:T(8,128)}, u32[]{:S(2)}) copy-start(f32[256,60,60]{0,2,1:T(8,128)} %reshape.244) | copy-start | bytes 11059204 | tf_op jit(solution)/shard_map/cond
  162.9 4.7 %copy-start = (f32[3,64,450]{2,1,0:T(8,128)S(1)}, f32[3,64,450]{2,1,0:T(8,128)}, u32[]{:S(2)}) copy-start(f32[3,64,450]{2,1,0:T(8,128)} %param.12) | copy-start | bytes 1036804
  162.9 138.0 %all-to-all-start.1 = ((f32[256,8,450]{0,2,1:T(8,128)}), f32[256,8,450]{0,2,1:T(8,128)}, u32[]{:S(2)}, u32[]{:S(2)}) async-start(f32[256,8,450]{0,2,1:T(8,128)} %all_to_all.33), calls=%async_computation.1 | async-start | bytes 7471104 | tf_op jit(solution)/shard_map/all_to_all | solution.py:107
  167.7 48.2 %collective-permute-start = (f32[3,64,4]{2,1,0:T(8,128)S(1)}, f32[3,64,4]{2,1,0:T(8,128)S(1)}, u32[]{:S(2)}, u32[]{:S(2)}) collective-permute-start(f32[3,64,4]{2,1,0:T(8,128)S(1)} %get-tuple-element.444), channel_id=1, source_target_pairs={{16,0},{32,16},{48,32},{64,48},{80,64},{96,80},{112,96},{0,112},{1... | collective-permute-start | bytes 9224 | tf_op jit(solution)/shard_map/while/body/eval_jaxpr/ppermute | solution.py:24
  173.3 44.7 %collective-permute-start.1 = (f32[3,64,4]{2,1,0:T(8,128)S(1)}, f32[3,64,4]{2,1,0:T(8,128)S(1)}, u32[]{:S(2)}, u32[]{:S(2)}) collective-permute-start(f32[3,64,4]{2,1,0:T(8,128)S(1)} %get-tuple-element.445), channel_id=1, source_target_pairs={{0,16},{16,32},{32,48},{48,64},{64,80},{80,96},{96,112},{112,0},{1... | collective-permute-start | bytes 9224 | tf_op jit(solution)/shard_map/while/body/eval_jaxpr/ppermute | solution.py:23
  218.1 3.0 collective-permute-start.2
  219.5 5.4 %collective-permute-start.3 = (f32[3,4,458]{2,1,0:T(4,128)S(1)}, f32[3,4,458]{2,1,0:T(4,128)S(1)}, u32[]{:S(2)}, u32[]{:S(2)}) collective-permute-start(f32[3,4,458]{2,1,0:T(4,128)S(1)} %get-tuple-element.447), channel_id=1, source_target_pairs={{0,1},{1,2},{2,3},{3,4},{4,5},{5,6},{6,7},{7,8},{8,9},{9,10},{10,1... | collective-permute-start | bytes 65960 | tf_op jit(solution)/shard_map/while/body/eval_jaxpr/ppermute | solution.py:23
  228.3 6.2 %collective-permute-start = (f32[3,64,4]{2,1,0:T(8,128)S(1)}, f32[3,64,4]{2,1,0:T(8,128)S(1)}, u32[]{:S(2)}, u32[]{:S(2)}) collective-permute-start(f32[3,64,4]{2,1,0:T(8,128)S(1)} %get-tuple-element.444), channel_id=1, source_target_pairs={{16,0},{32,16},{48,32},{64,48},{80,64},{96,80},{112,96},{0,112},{1... | collective-permute-start | bytes 9224 | tf_op jit(solution)/shard_map/while/body/eval_jaxpr/ppermute | solution.py:24
  229.6 8.2 %collective-permute-start.1 = (f32[3,64,4]{2,1,0:T(8,128)S(1)}, f32[3,64,4]{2,1,0:T(8,128)S(1)}, u32[]{:S(2)}, u32[]{:S(2)}) collective-permute-start(f32[3,64,4]{2,1,0:T(8,128)S(1)} %get-tuple-element.445), channel_id=1, source_target_pairs={{0,16},{16,32},{32,48},{48,64},{64,80},{80,96},{96,112},{112,0},{1... | collective-permute-start | bytes 9224 | tf_op jit(solution)/shard_map/while/body/eval_jaxpr/ppermute | solution.py:23
  238.0 1.6 collective-permute-start.2
  238.0 5.4 %collective-permute-start.3 = (f32[3,4,458]{2,1,0:T(4,128)S(1)}, f32[3,4,458]{2,1,0:T(4,128)S(1)}, u32[]{:S(2)}, u32[]{:S(2)}) collective-permute-start(f32[3,4,458]{2,1,0:T(4,128)S(1)} %get-tuple-element.447), channel_id=1, source_target_pairs={{0,1},{1,2},{2,3},{3,4},{4,5},{5,6},{6,7},{7,8},{8,9},{9,10},{10,1... | collective-permute-start | bytes 65960 | tf_op jit(solution)/shard_map/while/body/eval_jaxpr/ppermute | solution.py:23
  246.9 6.2 %collective-permute-start = (f32[3,64,4]{2,1,0:T(8,128)S(1)}, f32[3,64,4]{2,1,0:T(8,128)S(1)}, u32[]{:S(2)}, u32[]{:S(2)}) collective-permute-start(f32[3,64,4]{2,1,0:T(8,128)S(1)} %get-tuple-element.444), channel_id=1, source_target_pairs={{16,0},{32,16},{48,32},{64,48},{80,64},{96,80},{112,96},{0,112},{1... | collective-permute-start | bytes 9224 | tf_op jit(solution)/shard_map/while/body/eval_jaxpr/ppermute | solution.py:24
  248.0 8.2 %collective-permute-start.1 = (f32[3,64,4]{2,1,0:T(8,128)S(1)}, f32[3,64,4]{2,1,0:T(8,128)S(1)}, u32[]{:S(2)}, u32[]{:S(2)}) collective-permute-start(f32[3,64,4]{2,1,0:T(8,128)S(1)} %get-tuple-element.445), channel_id=1, source_target_pairs={{0,16},{16,32},{32,48},{48,64},{64,80},{80,96},{96,112},{112,0},{1... | collective-permute-start | bytes 9224 | tf_op jit(solution)/shard_map/while/body/eval_jaxpr/ppermute | solution.py:23
  256.4 1.6 collective-permute-start.2
  256.4 5.4 %collective-permute-start.3 = (f32[3,4,458]{2,1,0:T(4,128)S(1)}, f32[3,4,458]{2,1,0:T(4,128)S(1)}, u32[]{:S(2)}, u32[]{:S(2)}) collective-permute-start(f32[3,4,458]{2,1,0:T(4,128)S(1)} %get-tuple-element.447), channel_id=1, source_target_pairs={{0,1},{1,2},{2,3},{3,4},{4,5},{5,6},{6,7},{7,8},{8,9},{9,10},{10,1... | collective-permute-start | bytes 65960 | tf_op jit(solution)/shard_map/while/body/eval_jaxpr/ppermute | solution.py:23
  265.3 6.2 %collective-permute-start = (f32[3,64,4]{2,1,0:T(8,128)S(1)}, f32[3,64,4]{2,1,0:T(8,128)S(1)}, u32[]{:S(2)}, u32[]{:S(2)}) collective-permute-start(f32[3,64,4]{2,1,0:T(8,128)S(1)} %get-tuple-element.444), channel_id=1, source_target_pairs={{16,0},{32,16},{48,32},{64,48},{80,64},{96,80},{112,96},{0,112},{1... | collective-permute-start | bytes 9224 | tf_op jit(solution)/shard_map/while/body/eval_jaxpr/ppermute | solution.py:24
  265.4 8.3 %collective-permute-start.1 = (f32[3,64,4]{2,1,0:T(8,128)S(1)}, f32[3,64,4]{2,1,0:T(8,128)S(1)}, u32[]{:S(2)}, u32[]{:S(2)}) collective-permute-start(f32[3,64,4]{2,1,0:T(8,128)S(1)} %get-tuple-element.445), channel_id=1, source_target_pairs={{0,16},{16,32},{32,48},{48,64},{64,80},{80,96},{96,112},{112,0},{1... | collective-permute-start | bytes 9224 | tf_op jit(solution)/shard_map/while/body/eval_jaxpr/ppermute | solution.py:23
  273.8 1.6 collective-permute-start.2
  273.9 5.4 %collective-permute-start.3 = (f32[3,4,458]{2,1,0:T(4,128)S(1)}, f32[3,4,458]{2,1,0:T(4,128)S(1)}, u32[]{:S(2)}, u32[]{:S(2)}) collective-permute-start(f32[3,4,458]{2,1,0:T(4,128)S(1)} %get-tuple-element.447), channel_id=1, source_target_pairs={{0,1},{1,2},{2,3},{3,4},{4,5},{5,6},{6,7},{7,8},{8,9},{9,10},{10,1... | collective-permute-start | bytes 65960 | tf_op jit(solution)/shard_map/while/body/eval_jaxpr/ppermute | solution.py:23
  282.7 6.2 %collective-permute-start = (f32[3,64,4]{2,1,0:T(8,128)S(1)}, f32[3,64,4]{2,1,0:T(8,128)S(1)}, u32[]{:S(2)}, u32[]{:S(2)}) collective-permute-start(f32[3,64,4]{2,1,0:T(8,128)S(1)} %get-tuple-element.444), channel_id=1, source_target_pairs={{16,0},{32,16},{48,32},{64,48},{80,64},{96,80},{112,96},{0,112},{1... | collective-permute-start | bytes 9224 | tf_op jit(solution)/shard_map/while/body/eval_jaxpr/ppermute | solution.py:24
  282.8 8.3 %collective-permute-start.1 = (f32[3,64,4]{2,1,0:T(8,128)S(1)}, f32[3,64,4]{2,1,0:T(8,128)S(1)}, u32[]{:S(2)}, u32[]{:S(2)}) collective-permute-start(f32[3,64,4]{2,1,0:T(8,128)S(1)} %get-tuple-element.445), channel_id=1, source_target_pairs={{0,16},{16,32},{32,48},{48,64},{64,80},{80,96},{96,112},{112,0},{1... | collective-permute-start | bytes 9224 | tf_op jit(solution)/shard_map/while/body/eval_jaxpr/ppermute | solution.py:23
  291.2 1.6 collective-permute-start.2
  291.3 5.4 %collective-permute-start.3 = (f32[3,4,458]{2,1,0:T(4,128)S(1)}, f32[3,4,458]{2,1,0:T(4,128)S(1)}, u32[]{:S(2)}, u32[]{:S(2)}) collective-permute-start(f32[3,4,458]{2,1,0:T(4,128)S(1)} %get-tuple-element.447), channel_id=1, source_target_pairs={{0,1},{1,2},{2,3},{3,4},{4,5},{5,6},{6,7},{7,8},{8,9},{9,10},{10,1... | collective-permute-start | bytes 65960 | tf_op jit(solution)/shard_map/while/body/eval_jaxpr/ppermute | solution.py:23
where the time goes:
time: 319 us; the launch traced here: 315 us
  waiting for transfers between devices  133 us (42%)
  matrix products  77 us (24%)
  starting transfers between devices  46.1 us (14%)
  local copies, waits for them, and re-layouts  42.4 us (13%)
  other arithmetic  13.7 us (4%)
    ppermute x12, waiting for transfers between devices, with_halo(): before = lax.ppermute(last, axis, up)  74.5 us
    ppermute x12, waiting for transfers between devices, with_halo(): after = lax.ppermute(initial, axis, down)  58.6 us
    ppermute x12, starting transfers between devices, with_halo(): before = lax.ppermute(last, axis, up)  17.3 us
    ppermute x12, starting transfers between devices, with_halo(): after = lax.ppermute(initial, axis, down)  16 us
    all_to_all x2, local copies, waits for them, and re-layouts, body(): lax.all_to_all(flattened, 'lon', split_axis=0, concat_axis=1, tiled=True)  8.88 us
    all_to_all x1, starting transfers between devices, body(): lax.all_to_all(flattened, 'lon', split_axis=0, concat_axis=1, tiled=True)  8.19 us
    dot_general x1, matrix products, spectral_cut(): step_imag = -jnp.einsum('inb,nm->imb', grid, sin_first, precision=highest)  8.04 us
    dot_general x1, matrix products, spectral_cut(): step_real = jnp.einsum('inb,nm->imb', grid, cos_first, precision=highest)  7.78 us
  transfers between devices with their start and end apart: 26, of which 22 were waited for; matrix products, arithmetic and copies ran while one was open for 6% of the time, Pallas kernels for 0%

commit v1 on v0

v1 whole, which is shorter than its diff:
```python
import math

import jax
import jax.numpy as jnp
import ml_dtypes
import numpy as np
from jax import lax
from jax.experimental import pallas as pl
from jax.experimental.pallas import tpu as pltpu
from jax.sharding import PartitionSpec as P

MESH = pl.DeviceIdType.MESH
ANY = pl.ANY
VMEM = pltpu.VMEM

WAVE = 0.65
SUB = 20
POLE_DEV = 2
LON, LAT = 8, 16
ROWS, COLS = 64, 450
NLON = LON * COLS
NLAT = LAT * ROWS
LEV = 8
NF = 4
WIDE = 512
HALO = 24
EXT = ROWS + 2 * HALO
TILE = 8
LANE_TILES = ((0, 128), (128, 256), (256, 384), (384, COLS))


def tables():
    r = np.arange(COLS)
    angle = 2.0 * np.pi * ((r[:, None] * r[None, :]) % COLS) / COLS
    full = np.zeros((WIDE, 2 * WIDE), np.float64)
    full[:COLS, :COLS] = np.cos(angle)
    full[:COLS, WIDE : WIDE + COLS] = np.sin(angle)
    full = full.astype(np.float32)
    high = full.astype(ml_dtypes.bfloat16)
    low = (full - high.astype(np.float32)).astype(ml_dtypes.bfloat16)
    turn = 2.0 * np.pi * (np.arange(LON)[:, None] * r[None, :]) / NLON
    twist = np.zeros((2, LON, WIDE), np.float32)
    twist[0, :, :COLS] = np.cos(turn)
    twist[1, :, :COLS] = np.sin(turn)
    return high, low, twist


def butterflies(z, sign):
    n = len(z)
    if n == 1:
        return z
    even = butterflies(z[0::2], sign)
    odd = butterflies(z[1::2], sign)
    low, high = [], []
    for k in range(n // 2):
        er, ei = even[k]
        tr, ti = odd[k]
        if 4 * k == n:
            tr, ti = (-ti, tr) if sign > 0 else (ti, -tr)
        elif k:
            c = math.cos(2.0 * math.pi * k / n)
            s = sign * math.sin(2.0 * math.pi * k / n)
            tr, ti = c * tr - s * ti, c * ti + s * tr
        low.append((er + tr, ei + ti))
        high.append((er - tr, ei - ti))
    return low + high


def put_split(high_ref, low_ref, row, lanes, value):
    top = value.astype(jnp.bfloat16)
    high_ref[row : row + 16, lanes[0] : lanes[1]] = top
    low_ref[row : row + 16, lanes[0] : lanes[1]] = (value - top.astype(jnp.float32)).astype(jnp.bfloat16)


def multiply(high_ref, low_ref, wh_ref, wl_ref, out_ref):
    for block in range(4):
        cols = slice(block * 256, (block + 1) * 256)
        out_ref[:, cols] = (
            jnp.dot(high_ref[...], wh_ref[:, cols], preferred_element_type=jnp.float32)
            + jnp.dot(low_ref[...], wh_ref[:, cols], preferred_element_type=jnp.float32)
            + jnp.dot(high_ref[...], wl_ref[:, cols], preferred_element_type=jnp.float32)
        )


def filter_chunk(j, recv, back, twist, mask, yh, yl, wh, wl, prod):
    for lo, hi in LANE_TILES:
        z = []
        for d in range(LON):
            re = recv[j, d, 0:2, :, lo:hi].reshape(16, hi - lo)
            im = recv[j, d, 2:4, :, lo:hi].reshape(16, hi - lo)
            z.append((re, im))
        y = butterflies(z, -1)
        for s in range(LON):
            re, im = y[s]
            if s:
                c = twist[0, s : s + 1, lo:hi]
                n = twist[1, s : s + 1, lo:hi]
                re, im = re * c + im * n, im * c - re * n
            put_split(yh, yl, s * 32, (lo, hi), re)
            put_split(yh, yl, s * 32 + 16, (lo, hi), im)
    multiply(yh, yl, wh, wl, prod)
    for lo, hi in LANE_TILES:
        for s in range(LON):
            a = slice(s * 32, s * 32 + 16)
            b = slice(s * 32 + 16, s * 32 + 32)
            keep = mask[s, :, lo:hi]
            re = (prod[a, lo:hi] + prod[b, WIDE + lo : WIDE + hi]) * keep
            im = (prod[b, lo:hi] - prod[a, WIDE + lo : WIDE + hi]) * keep
            put_split(yh, yl, s * 32, (lo, hi), re)
            put_split(yh, yl, s * 32 + 16, (lo, hi), im)
    multiply(yh, yl, wh, wl, prod)
    for lo, hi in LANE_TILES:
        z = []
        for s in range(LON):
            a = slice(s * 32, s * 32 + 16)
            b = slice(s * 32 + 16, s * 32 + 32)
            re = prod[a, lo:hi] - prod[b, WIDE + lo : WIDE + hi]
            im = prod[b, lo:hi] + prod[a, WIDE + lo : WIDE + hi]
            if s:
                c = twist[0, s : s + 1, lo:hi]
                n = twist[1, s : s + 1, lo:hi]
                re, im = re * c - im * n, im * c + re * n
            z.append((re, im))
        x = butterflies(z, 1)
        for d in range(LON):
            back[j, d, 0:2, :, lo:hi] = x[d][0].reshape(2, 8, hi - lo)
            back[j, d, 2:4, :, lo:hi] = x[d][1].reshape(2, 8, hi - lo)


def wave_kernel(
    fields, baro, land, cutoff, wh_hbm, wl_hbm, twist,
    filt, state_out, open_out,
    recv, back, wh, wl, yh, yl, prod, mask,
    own, own_land, src4, st_c, st_l, st_r, ext, opens, res_state, res_open,
    fwd_send, fwd_recv, ret_send, ret_recv, halo_send, halo_recv, local_sem,
):
    lon = lax.axis_index("lon")
    lat = lax.axis_index("lat")
    polar = (lat < POLE_DEV) | (lat >= LAT - POLE_DEV)
    partner = lax.rem(lat + LAT // 2, LAT)
    worker = (partner < POLE_DEV) | (partner >= LAT - POLE_DEV)

    load_state = pltpu.make_async_copy(baro, own, local_sem.at[0])
    load_land = pltpu.make_async_copy(land, own_land, local_sem.at[1])
    load_state.start()
    load_land.start()
    load_wh = pltpu.make_async_copy(wh_hbm, wh, local_sem.at[2])
    load_wl = pltpu.make_async_copy(wl_hbm, wl, local_sem.at[3])

    @pl.when(worker)
    def _():
        load_wh.start()
        load_wl.start()

    def near(dx, dy):
        return {"lon": lax.rem(lon + dx + LON, LON), "lat": lax.rem(lat + dy + LAT, LAT)}

    sides = [(dx, dy) for dx in (-1, 0, 1) for dy in (-1, 0, 1) if (dx, dy) != (0, 0)]
    barrier = pltpu.get_barrier_semaphore()
    for dx, dy in sides:
        pl.semaphore_signal(barrier, inc=1, device_id=near(dx, dy), device_id_type=MESH)

    @pl.when(polar | worker)
    def _():
        def greet(t, _):
            pl.semaphore_signal(barrier, inc=1, device_id={"lon": t, "lat": partner}, device_id_type=MESH)
            return 0

        lax.fori_loop(0, LON, greet, 0)
        pl.semaphore_wait(barrier, len(sides) + LON)

    @pl.when(jnp.logical_not(polar | worker))
    def _():
        pl.semaphore_wait(barrier, len(sides))

    def send_level(j, _):
        def send_one(t, _):
            pltpu.make_async_remote_copy(
                src_ref=fields.at[:, j, pl.ds(pl.multiple_of(t * TILE, TILE), TILE), :],
                dst_ref=recv.at[j, lon],
                send_sem=fwd_send,
                recv_sem=fwd_recv.at[j],
                device_id={"lon": t, "lat": partner},
                device_id_type=MESH,
            ).start()
            return 0

        lax.fori_loop(0, LON, send_one, 0)
        return 0

    @pl.when(polar)
    def _():
        send_level(0, 0)

    load_state.wait()
    load_land.wait()
    for c in range(3):
        src4[c, :, 0:384] = own[c, :, 0:384]
        src4[c, :, 384:COLS] = own[c, :, 384:COLS]
    src4[3, :, 0:384] = own_land[:, 0:384].astype(jnp.float32)
    src4[3, :, 384:COLS] = own_land[:, 384:COLS].astype(jnp.float32)
    zero_pad = jnp.zeros((4, ROWS, WIDE - COLS), jnp.float32)
    src4[:, :, COLS:WIDE] = zero_pad

    row_src = {1: slice(ROWS - HALO, ROWS), 0: slice(0, ROWS), -1: slice(0, HALO)}
    row_dst = {1: slice(0, HALO), 0: slice(HALO, HALO + ROWS), -1: slice(HALO + ROWS, EXT)}
    copies = []
    for n, (dx, dy) in enumerate(sides):
        if dx == 0:
            src = src4.at[:, row_src[dy], :]
            dst = st_c.at[:, row_dst[dy], :]
        elif dx == 1:
            src = src4.at[:, row_src[dy], 384:512]
            dst = st_l.at[:, row_dst[dy], :]
        else:
            src = src4.at[:, row_src[dy], 0:128]
            dst = st_r.at[:, row_dst[dy], :]
        copy = pltpu.make_async_remote_copy(
            src_ref=src, dst_ref=dst, send_sem=halo_send.at[n], recv_sem=halo_recv.at[n],
            device_id=near(dx, dy), device_id_type=MESH,
        )
        copy.start()
        copies.append(copy)

    @pl.when(polar)
    def _():
        lax.fori_loop(1, LEV, send_level, 0)

    st_c[:, HALO : HALO + ROWS, :] = src4[...]
    for copy in copies:
        copy.wait()

    lane128 = lax.broadcasted_iota(jnp.int32, (EXT, 128), 1)
    for c in range(4):
        mid = pltpu.roll(st_c[c], HALO, 1)
        ext[c, :, 128:384] = mid[:, 128:384]
        left = pltpu.roll(st_l[c], 128 - (COLS - HALO - 384), 1)
        ext[c, :, 0:128] = jnp.where(lane128 < HALO, left, mid[:, 0:128])
        right = pltpu.roll(st_r[c], HALO + COLS - 384, 1)
        ext[c, :, 384:512] = jnp.where(lane128 >= HALO + COLS - 384, right, mid[:, 384:512])

    ocean = ext[3]
    row_id = lax.rem(lat * ROWS - HALO + NLAT + lax.broadcasted_iota(jnp.int32, (EXT, WIDE), 0), NLAT)
    east_open = ocean * pltpu.roll(ocean, WIDE - 1, 1)
    north_open = jnp.where(row_id == NLAT - 1, 0.0, ocean * pltpu.roll(ocean, EXT - 1, 0))
    opens[0] = east_open
    opens[1] = north_open
    ext[1] = ext[1] * east_open
    ext[2] = ext[2] * north_open
    ext[3] = WAVE * ocean

    def subcycle(_, carry):
        east = ext[1]
        north = ext[2]
        div = east - pltpu.roll(east, 1, 1) + north - pltpu.roll(north, 1, 0)
        surface = ext[0] - ext[3] * div
        ext[0] = surface
        ext[1] = opens[0] * (east - WAVE * (pltpu.roll(surface, WIDE - 1, 1) - surface))
        ext[2] = opens[1] * (north - WAVE * (pltpu.roll(surface, EXT - 1, 0) - surface))
        return carry

    lax.fori_loop(0, SUB, subcycle, 0)

    inner = slice(HALO, HALO + ROWS)
    for c in range(3):
        moved = pltpu.roll(ext[c, inner, :], WIDE - HALO, 1)
        res_state[c] = moved[:, :COLS]
    for c in range(2):
        moved = pltpu.roll(opens[c, inner, :], WIDE - HALO, 1)
        res_open[c] = moved[:, :COLS]
    save_state = pltpu.make_async_copy(res_state, state_out, local_sem.at[0])
    save_open = pltpu.make_async_copy(res_open, open_out, local_sem.at[1])
    save_state.start()
    save_open.start()

    @pl.when(worker)
    def _():
        load_wh.wait()
        load_wl.wait()
        top = jnp.where(partner < POLE_DEV, partner, partner - (LAT - 2 * POLE_DEV))
        first = top * ROWS + lon * TILE
        sub = lax.rem(lax.broadcasted_iota(jnp.int32, (16, WIDE), 0), TILE)
        wave = LON * lax.broadcasted_iota(jnp.int32, (16, WIDE), 1)
        limit = jnp.zeros((16, WIDE), jnp.int32)
        for i in range(TILE):
            limit = jnp.where(sub == i, cutoff[first + i], limit)
        for s in range(LON):
            m = wave + s
            folded = jnp.minimum(m, NLON - m)
            mask[s] = jnp.where(folded <= limit, 1.0 / NLON, 0.0)
        yh[...] = jnp.zeros_like(yh)
        yl[...] = jnp.zeros_like(yl)

        def chunk(j, _):
            pltpu.make_async_copy(recv.at[j], recv.at[j], fwd_recv.at[j]).wait()
            filter_chunk(j, recv, back, twist, mask, yh, yl, wh, wl, prod)

            def reply(d, _):
                pltpu.make_async_remote_copy(
                    src_ref=back.at[j, d],
                    dst_ref=filt.at[:, j, pl.ds(pl.multiple_of(lon * TILE, TILE), TILE), :],
                    send_sem=ret_send,
                    recv_sem=ret_recv,
                    device_id={"lon": d, "lat": partner},
                    device_id_type=MESH,
                ).start()
                return 0

            lax.fori_loop(0, LON, reply, 0)
            return 0

        lax.fori_loop(0, LEV, chunk, 0)
        pltpu.make_async_copy(back, back, ret_send).wait()

    @pl.when(polar)
    def _():
        pltpu.make_async_copy(fields, fields, fwd_send).wait()
        pltpu.make_async_copy(filt, filt, ret_recv).wait()

    save_state.wait()
    save_open.wait()


def final_kernel(polar, thick, fields, filt, state, opens, tracers, velocity, sea):
    total = thick[0]
    for k in range(1, LEV):
        total = total + thick[k]
    sea[...] = state[0]

    def finish(source):
        tracers[...] = source[0:2]
        for c in range(2):
            column = None
            for k in range(LEV):
                term = (thick[k] / total) * source[2 + c, k]
                column = term if column is None else column + term
            shift = state[1 + c] - column
            gate = opens[c]
            for k in range(LEV):
                velocity[c, k] = gate * (source[2 + c, k] + shift)

    @pl.when(polar[0] == 1)
    def _():
        finish(filt)

    @pl.when(polar[0] == 0)
    def _():
        finish(fields)


def body(fields, thickness, cutoff, barotropic, land_sea):
    f32 = jnp.float32
    high, low, twist = tables()
    sds = jax.ShapeDtypeStruct
    filt, state, opens = pl.pallas_call(
        wave_kernel,
        out_shape=(
            sds((NF, LEV, ROWS, COLS), f32),
            sds((3, ROWS, COLS), f32),
            sds((2, ROWS, COLS), f32),
        ),
        in_specs=[
            pl.BlockSpec(memory_space=ANY),
            pl.BlockSpec(memory_space=ANY),
            pl.BlockSpec(memory_space=ANY),
            pl.BlockSpec(memory_space=pltpu.SMEM),
            pl.BlockSpec(memory_space=ANY),
            pl.BlockSpec(memory_space=ANY),
            pl.BlockSpec(memory_space=VMEM),
        ],
        out_specs=[pl.BlockSpec(memory_space=ANY)] * 3,
        scratch_shapes=[
            VMEM((LEV, LON, NF, TILE, COLS), f32),
            VMEM((LEV, LON, NF, TILE, COLS), f32),
            VMEM((WIDE, 2 * WIDE), jnp.bfloat16),
            VMEM((WIDE, 2 * WIDE), jnp.bfloat16),
            VMEM((256, WIDE), jnp.bfloat16),
            VMEM((256, WIDE), jnp.bfloat16),
            VMEM((256, 2 * WIDE), f32),
            VMEM((LON, 16, WIDE), f32),
            VMEM((3, ROWS, COLS), f32),
            VMEM((ROWS, COLS), jnp.int32),
            VMEM((4, ROWS, WIDE), f32),
            VMEM((4, EXT, WIDE), f32),
            VMEM((4, EXT, 128), f32),
            VMEM((4, EXT, 128), f32),
            VMEM((4, EXT, WIDE), f32),
            VMEM((2, EXT, WIDE), f32),
            VMEM((3, ROWS, COLS), f32),
            VMEM((2, ROWS, COLS), f32),
            pltpu.SemaphoreType.DMA,
            pltpu.SemaphoreType.DMA((LEV,)),
            pltpu.SemaphoreType.DMA,
            pltpu.SemaphoreType.DMA,
            pltpu.SemaphoreType.DMA((8,)),
            pltpu.SemaphoreType.DMA((8,)),
            pltpu.SemaphoreType.DMA((4,)),
        ],
        compiler_params=pltpu.CompilerParams(
            collective_id=0, has_side_effects=True, vmem_limit_bytes=60 * 1024 * 1024
        ),
        name="wave",
    )(fields, barotropic, land_sea, cutoff, jnp.asarray(high), jnp.asarray(low), jnp.asarray(twist))

    lat = lax.axis_index("lat")
    polar = ((lat < POLE_DEV) | (lat >= LAT - POLE_DEV)).astype(jnp.int32).reshape(1)
    rows = lambda i, p: (0, i, 0)
    return tuple(
        pl.pallas_call(
            final_kernel,
            out_shape=(
                sds((2, LEV, ROWS, COLS), f32),
                sds((2, LEV, ROWS, COLS), f32),
                sds((ROWS, COLS), f32),
            ),
            grid_spec=pltpu.PrefetchScalarGridSpec(
                num_scalar_prefetch=1,
                grid=(ROWS // TILE,),
                in_specs=[
                    pl.BlockSpec(memory_space=pltpu.SMEM),
                    pl.BlockSpec((NF, LEV, TILE, COLS), lambda i, p: (0, 0, i * (1 - p[0]), 0)),
                    pl.BlockSpec((NF, LEV, TILE, COLS), lambda i, p: (0, 0, i * p[0], 0)),
                    pl.BlockSpec((3, TILE, COLS), rows),
                    pl.BlockSpec((2, TILE, COLS), rows),
                ],
                out_specs=[
                    pl.BlockSpec((2, LEV, TILE, COLS), lambda i, p: (0, 0, i, 0)),
                    pl.BlockSpec((2, LEV, TILE, COLS), lambda i, p: (0, 0, i, 0)),
                    pl.BlockSpec((TILE, COLS), lambda i, p: (i, 0)),
                ],
            ),
            name="final",
        )(polar, thickness, fields, filt, state, opens)
    )


def solution(mesh):
    return jax.shard_map(
        body,
        mesh=mesh,
        in_specs=(P(None, None, "lat", "lon"), P(), P(), P(None, "lat", "lon"), P("lat", "lon")),
        out_specs=(P(None, None, "lat", "lon"), P(None, None, "lat", "lon"), P("lat", "lon")),
        check_vma=False,
    )
```

time: 319 us -> 96.5 us (0.30)
  the two profiles are of different devices: /device:TPU:0 before, /device:TPU:97 now
where the time goes in v1:
time: 96.5 us; the launch traced here: 96.2 us
  Pallas kernels  95.6 us (99%)
    pallas_call x1, Pallas kernels, body(): pl.pallas_call(wave_kernel, out_shape=(sds((NF, LEV, ROWS, COLS), f32), s...  88.4 us
    pallas_call x1, Pallas kernels, body(): pl.pallas_call(final_kernel, out_shape=(sds((2, LEV, ROWS, COLS), f32), s...  7.14 us

profile of v1, /device:TPU:97, one launch (start us, length us, event | category | flops | bytes accessed | tf_op | source)
XLA Modules:
  0.0 96.2 jit_solution(17811386551391525578)
XLA Ops:
  0.6 88.4 %wave.1 = (f32[4,8,64,450]{3,2,1,0:T(8,128)}, f32[3,64,450]{2,1,0:T(8,128)}, f32[2,64,450]{2,1,0:T(8,128)}) custom-call(f32[4,8,64,450]{3,2,1,0:T(8,128)} %fields.3, f32[3,64,450]{2,1,0:T(8,128)} %baro.1, s32[64,450]{1,0:T(8,128)} %land.1, s32[256]{0:T(256)} %cutoff.1, bf16[512,1024]{1,0:T(8,128)(2,1)} %constant.14.clone.wh_hbm, ...), custom_call_target="tpu_custom_call" | custom-call | tf_op jit(solution)/shard_map/wave/pallas_call | solution.py:355
  89.1 7.1 %final.1 = (f32[2,8,64,450]{3,2,1,0:T(8,128)}, f32[2,8,64,450]{3,2,1,0:T(8,128)}, f32[64,450]{1,0:T(8,128)}) custom-call(s32[1]{0:T(128)} %bitcast.polar, f32[8]{0:T(128)} %thick.1, f32[4,8,64,450]{3,2,1,0:T(8,128)} %fields.3, f32[4,8,64,450]{3,2,1,0:T(8,128)} %get-tuple-element.6.filt, f32[3,64,450]{2,1,0:T(8,128)} %get-tuple-element.7.state, ...), custom_call_target="tpu_custom_call" | custom-call | tf_op jit(solution)/shard_map/final/pallas_call | solution.py:409

commit v2 on v1

--- a/solution.py
+++ b/solution.py
@@ -26,6 +26,8 @@
 HALO = 24
 EXT = ROWS + 2 * HALO
 TILE = 8
+NEAR_LEV = 6
+PER_CHUNK = 4
 LANE_TILES = ((0, 128), (128, 256), (256, 384), (384, COLS))
 
 
@@ -130,15 +132,24 @@
 def wave_kernel(
     fields, baro, land, cutoff, wh_hbm, wl_hbm, twist,
     filt, state_out, open_out,
-    recv, back, wh, wl, yh, yl, prod, mask,
-    own, own_land, src4, st_c, st_l, st_r, ext, opens, res_state, res_open,
-    fwd_send, fwd_recv, ret_send, ret_recv, halo_send, halo_recv, local_sem,
+    recv, back, relay, wh, wl, yh, yl, prod, mask,
+    own, own_land, src4, edge_r, edge_l, st_c, st_l, st_r, ext, opens, res_state, res_open,
+    fwd_send, fwd_recv, ret_send, ret_recv, relay_recv, relay_send, halo_send, halo_recv, local_sem,
 ):
     lon = lax.axis_index("lon")
     lat = lax.axis_index("lat")
-    polar = (lat < POLE_DEV) | (lat >= LAT - POLE_DEV)
-    partner = lax.rem(lat + LAT // 2, LAT)
-    worker = (partner < POLE_DEV) | (partner >= LAT - POLE_DEV)
+    pair = lat // 2
+    core = lax.rem(lat, 2)
+    north = lax.rem(pair, 4) < 2
+    polar = (pair == 0) | (pair == 7)
+    near_y = (pair == 3) | (pair == 4)
+    relays = (pair == 1) | (pair == 6)
+    far = (pair == 2) | (pair == 5)
+    worker = near_y | far
+    home = jnp.where(north, 0, LAT - 2) + core
+    y_lat = jnp.where(north, 8, 6) + core
+    relay_lat = jnp.where(north, 2, 12) + core
+    far_lat = jnp.where(north, 10, 4) + core
 
     load_state = pltpu.make_async_copy(baro, own, local_sem.at[0])
     load_land = pltpu.make_async_copy(land, own_land, local_sem.at[1])
@@ -152,45 +163,56 @@
         load_wh.start()
         load_wl.start()
 
+    sides = [(dx, dy) for dy in (0, 1, -1) for dx in (-1, 0, 1) if (dx, dy) != (0, 0)]
+
     def near(dx, dy):
         return {"lon": lax.rem(lon + dx + LON, LON), "lat": lax.rem(lat + dy + LAT, LAT)}
 
-    sides = [(dx, dy) for dx in (-1, 0, 1) for dy in (-1, 0, 1) if (dx, dy) != (0, 0)]
+    def inside(dy):
+        return lat < LAT - 1 if dy > 0 else lat > 0
+
+    def when_inside(dy, action):
+        if dy == 0:
+            action()
+        else:
+            pl.when(inside(dy))(action)
+
     barrier = pltpu.get_barrier_semaphore()
+
+    def greet_at(lon_index, lat_index):
+        pl.semaphore_signal(
+            barrier, inc=1, device_id={"lon": lon_index, "lat": lat_index}, device_id_type=MESH
+        )
+
+    def greet_row(lat_index):
+        def one(t, _):
+            greet_at(t, lat_index)
+            return 0
+
+        lax.fori_loop(0, LON, one, 0)
+
     for dx, dy in sides:
-        pl.semaphore_signal(barrier, inc=1, device_id=near(dx, dy), device_id_type=MESH)
-
-    @pl.when(polar | worker)
-    def _():
-        def greet(t, _):
-            pl.semaphore_signal(barrier, inc=1, device_id={"lon": t, "lat": partner}, device_id_type=MESH)
-            return 0
-
-        lax.fori_loop(0, LON, greet, 0)
-        pl.semaphore_wait(barrier, len(sides) + LON)
-
-    @pl.when(jnp.logical_not(polar | worker))
-    def _():
-        pl.semaphore_wait(barrier, len(sides))
-
-    def send_level(j, _):
-        def send_one(t, _):
-            pltpu.make_async_remote_copy(
-                src_ref=fields.at[:, j, pl.ds(pl.multiple_of(t * TILE, TILE), TILE), :],
-                dst_ref=recv.at[j, lon],
-                send_sem=fwd_send,
-                recv_sem=fwd_recv.at[j],
-                device_id={"lon": t, "lat": partner},
-                device_id_type=MESH,
-            ).start()
-            return 0
-
-        lax.fori_loop(0, LON, send_one, 0)
-        return 0
+        when_inside(dy, lambda dx=dx, dy=dy: greet_at(near(dx, dy)["lon"], near(dx, dy)["lat"]))
 
     @pl.when(polar)
     def _():
-        send_level(0, 0)
+        greet_row(y_lat)
+        greet_row(far_lat)
+        greet_at(lon, relay_lat)
+
+    @pl.when(near_y)
+    def _():
+        greet_row(home)
+
+    @pl.when(far)
+    def _():
+        greet_row(home)
+        greet_row(relay_lat)
+
+    @pl.when(relays)
+    def _():
+        greet_row(far_lat)
+        greet_at(lon, home)
 
     load_state.wait()
     load_land.wait()
@@ -199,8 +221,43 @@
         src4[c, :, 384:COLS] = own[c, :, 384:COLS]
     src4[3, :, 0:384] = own_land[:, 0:384].astype(jnp.float32)
     src4[3, :, 384:COLS] = own_land[:, 384:COLS].astype(jnp.float32)
-    zero_pad = jnp.zeros((4, ROWS, WIDE - COLS), jnp.float32)
-    src4[:, :, COLS:WIDE] = zero_pad
+    src4[:, :, COLS:WIDE] = jnp.zeros((4, ROWS, WIDE - COLS), jnp.float32)
+    st_c[:, HALO : HALO + ROWS, :] = src4[...]
+    lane = lax.broadcasted_iota(jnp.int32, (ROWS, 128), 1)
+    right_pack = jnp.zeros((ROWS, 128), jnp.float32)
+    left_pack = right_pack
+    for c in range(4):
+        here = (lane >= c * HALO) & (lane < (c + 1) * HALO)
+        right_edge = pltpu.roll(src4[c, :, 384:512], (c * HALO - (COLS - HALO - 384)) % 128, 1)
+        left_edge = src4[c, :, 0:128]
+        if c:
+            left_edge = pltpu.roll(left_edge, c * HALO, 1)
+        right_pack = jnp.where(here, right_edge, right_pack)
+        left_pack = jnp.where(here, left_edge, left_pack)
+    edge_r[...] = right_pack
+    edge_l[...] = left_pack
+
+    full = len(sides) - jnp.where((lat == 0) | (lat == LAT - 1), 3, 0)
+    extra = jnp.where(polar, 2 * LON + 1, jnp.where(near_y, LON, jnp.where(far, 2 * LON, LON + 1)))
+    pl.semaphore_wait(barrier, full + extra)
+
+    def send_level(level, slot, lat_index):
+        def send_one(t, _):
+            pltpu.make_async_remote_copy(
+                src_ref=fields.at[:, level, pl.ds(pl.multiple_of(t * TILE, TILE), TILE), :],
+                dst_ref=recv.at[slot, lon],
+                send_sem=fwd_send,
+                recv_sem=fwd_recv.at[slot],
+                device_id={"lon": t, "lat": lat_index},
+                device_id_type=MESH,
+            ).start()
+            return 0
+
+        lax.fori_loop(0, LON, send_one, 0)
+
+    @pl.when(polar)
+    def _():
+        send_level(0, 0, y_lat)
 
     row_src = {1: slice(ROWS - HALO, ROWS), 0: slice(0, ROWS), -1: slice(0, HALO)}
     row_dst = {1: slice(0, HALO), 0: slice(HALO, HALO + ROWS), -1: slice(HALO + ROWS, EXT)}
@@ -209,38 +266,52 @@
         if dx == 0:
             src = src4.at[:, row_src[dy], :]
             dst = st_c.at[:, row_dst[dy], :]
-        elif dx == 1:
-            src = src4.at[:, row_src[dy], 384:512]
-            dst = st_l.at[:, row_dst[dy], :]
         else:
-            src = src4.at[:, row_src[dy], 0:128]
-            dst = st_r.at[:, row_dst[dy], :]
+            src = (edge_r if dx == 1 else edge_l).at[row_src[dy], :]
+            dst = (st_l if dx == 1 else st_r).at[row_dst[dy], :]
         copy = pltpu.make_async_remote_copy(
             src_ref=src, dst_ref=dst, send_sem=halo_send.at[n], recv_sem=halo_recv.at[n],
             device_id=near(dx, dy), device_id_type=MESH,
         )
-        copy.start()
-        copies.append(copy)
+        when_inside(dy, copy.start)
+        copies.append((dy, copy))
 
     @pl.when(polar)
     def _():
-        lax.fori_loop(1, LEV, send_level, 0)
-
-    st_c[:, HALO : HALO + ROWS, :] = src4[...]
-    for copy in copies:
-        copy.wait()
-
-    lane128 = lax.broadcasted_iota(jnp.int32, (EXT, 128), 1)
+        for level in range(NEAR_LEV, LEV):
+            send_level(level, level - NEAR_LEV, far_lat)
+            step = level - NEAR_LEV
+            send_level(1 + step, 1 + step, y_lat)
+
+        def more(level, _):
+            send_level(level, level, y_lat)
+            return 0
+
+        lax.fori_loop(1 + LEV - NEAR_LEV, NEAR_LEV, more, 0)
+
+    for dy, copy in copies:
+        when_inside(dy, copy.wait_send)
+        when_inside(-dy, copy.wait_recv)
+    for dy in (1, -1):
+        @pl.when(jnp.logical_not(inside(-dy)))
+        def _(dy=dy):
+            st_c[:, row_dst[dy], :] = jnp.zeros((4, HALO, WIDE), jnp.float32)
+            st_l[row_dst[dy], :] = jnp.zeros((HALO, 128), jnp.float32)
+            st_r[row_dst[dy], :] = jnp.zeros((HALO, 128), jnp.float32)
+
+    lane_ext = lax.broadcasted_iota(jnp.int32, (EXT, 128), 1)
+    edge = HALO + COLS - 384
     for c in range(4):
         mid = pltpu.roll(st_c[c], HALO, 1)
         ext[c, :, 128:384] = mid[:, 128:384]
-        left = pltpu.roll(st_l[c], 128 - (COLS - HALO - 384), 1)
-        ext[c, :, 0:128] = jnp.where(lane128 < HALO, left, mid[:, 0:128])
-        right = pltpu.roll(st_r[c], HALO + COLS - 384, 1)
-        ext[c, :, 384:512] = jnp.where(lane128 >= HALO + COLS - 384, right, mid[:, 384:512])
+        left = pltpu.roll(st_l[...], 128 - c * HALO, 1) if c else st_l[...]
+        ext[c, :, 0:128] = jnp.where(lane_ext < HALO, left, mid[:, 0:128])
+        right = pltpu.roll(st_r[...], (edge - c * HALO) % 128, 1)
+        right = jnp.where(lane_ext < edge + HALO, right, 0.0)
+        ext[c, :, 384:512] = jnp.where(lane_ext >= edge, right, mid[:, 384:512])
 
     ocean = ext[3]
-    row_id = lax.rem(lat * ROWS - HALO + NLAT + lax.broadcasted_iota(jnp.int32, (EXT, WIDE), 0), NLAT)
+    row_id = lat * ROWS - HALO + lax.broadcasted_iota(jnp.int32, (EXT, WIDE), 0)
     east_open = ocean * pltpu.roll(ocean, WIDE - 1, 1)
     north_open = jnp.where(row_id == NLAT - 1, 0.0, ocean * pltpu.roll(ocean, EXT - 1, 0))
     opens[0] = east_open
@@ -259,7 +330,66 @@
         ext[2] = opens[1] * (north - WAVE * (pltpu.roll(surface, EXT - 1, 0) - surface))
         return carry
 
-    lax.fori_loop(0, SUB, subcycle, 0)
+    chunks = jnp.where(near_y, NEAR_LEV, jnp.where(far, LEV - NEAR_LEV, 0))
+
+    @pl.when(worker)
+    def _():
+        load_wh.wait()
+        load_wl.wait()
+        first = (jnp.where(north, 0, 2) + core) * ROWS + lon * TILE
+        sub = lax.rem(lax.broadcasted_iota(jnp.int32, (16, WIDE), 0), TILE)
+        wave = LON * lax.broadcasted_iota(jnp.int32, (16, WIDE), 1)
+        limit = jnp.zeros((16, WIDE), jnp.int32)
+        for i in range(TILE):
+            limit = jnp.where(sub == i, cutoff[first + i], limit)
+        for s in range(LON):
+            m = wave + s
+            folded = jnp.minimum(m, NLON - m)
+            mask[s] = jnp.where(folded <= limit, 1.0 / NLON, 0.0)
+        yh[...] = jnp.zeros_like(yh)
+        yl[...] = jnp.zeros_like(yl)
+
+        def chunk(j, _):
+            pltpu.make_async_copy(recv.at[j], recv.at[j], fwd_recv.at[j]).wait()
+            filter_chunk(j, recv, back, twist, mask, yh, yl, wh, wl, prod)
+
+            @pl.when(near_y)
+            def _():
+                def reply(d, _):
+                    pltpu.make_async_remote_copy(
+                        src_ref=back.at[j, d],
+                        dst_ref=filt.at[:, j, pl.ds(pl.multiple_of(lon * TILE, TILE), TILE), :],
+                        send_sem=ret_send.at[j],
+                        recv_sem=ret_recv,
+                        device_id={"lon": d, "lat": home},
+                        device_id_type=MESH,
+                    ).start()
+                    return 0
+
+                lax.fori_loop(0, LON, reply, 0)
+
+            @pl.when(far)
+            def _():
+                def reply(d, _):
+                    pltpu.make_async_remote_copy(
+                        src_ref=back.at[j, d],
+                        dst_ref=relay.at[j, lon],
+                        send_sem=ret_send.at[j],
+                        recv_sem=relay_recv.at[j, lon],
+                        device_id={"lon": d, "lat": relay_lat},
+                        device_id_type=MESH,
+                    ).start()
+                    return 0
+
+                lax.fori_loop(0, LON, reply, 0)
+
+            lax.fori_loop(0, jnp.where(j < SUB // PER_CHUNK, PER_CHUNK, 0), subcycle, 0)
+            return 0
+
+        lax.fori_loop(0, chunks, chunk, 0)
+
+    left_over = SUB - PER_CHUNK * jnp.minimum(chunks, SUB // PER_CHUNK)
+    lax.fori_loop(0, left_over, subcycle, 0)
 
     inner = slice(HALO, HALO + ROWS)
     for c in range(3):
@@ -273,44 +403,32 @@
     save_state.start()
     save_open.start()
 
-    @pl.when(worker)
-    def _():
-        load_wh.wait()
-        load_wl.wait()
-        top = jnp.where(partner < POLE_DEV, partner, partner - (LAT - 2 * POLE_DEV))
-        first = top * ROWS + lon * TILE
-        sub = lax.rem(lax.broadcasted_iota(jnp.int32, (16, WIDE), 0), TILE)
-        wave = LON * lax.broadcasted_iota(jnp.int32, (16, WIDE), 1)
-        limit = jnp.zeros((16, WIDE), jnp.int32)
-        for i in range(TILE):
-            limit = jnp.where(sub == i, cutoff[first + i], limit)
-        for s in range(LON):
-            m = wave + s
-            folded = jnp.minimum(m, NLON - m)
-            mask[s] = jnp.where(folded <= limit, 1.0 / NLON, 0.0)
-        yh[...] = jnp.zeros_like(yh)
-        yl[...] = jnp.zeros_like(yl)
-
-        def chunk(j, _):
-            pltpu.make_async_copy(recv.at[j], recv.at[j], fwd_recv.at[j]).wait()
-            filter_chunk(j, recv, back, twist, mask, yh, yl, wh, wl, prod)
-
-            def reply(d, _):
+    @pl.when(relays)
+    def _():
+        for j in range(LEV - NEAR_LEV):
+            def pass_on(t, _, j=j):
+                here = relay.at[j, t]
+                pltpu.make_async_copy(here, here, relay_recv.at[j, t]).wait()
                 pltpu.make_async_remote_copy(
-                    src_ref=back.at[j, d],
-                    dst_ref=filt.at[:, j, pl.ds(pl.multiple_of(lon * TILE, TILE), TILE), :],
-                    send_sem=ret_send,
+                    src_ref=here,
+                    dst_ref=filt.at[:, NEAR_LEV + j, pl.ds(pl.multiple_of(t * TILE, TILE), TILE), :],
+                    send_sem=relay_send,
                     recv_sem=ret_recv,
-                    device_id={"lon": d, "lat": partner},
+                    device_id={"lon": lon, "lat": home},
                     device_id_type=MESH,
                 ).start()
                 return 0
 
-            lax.fori_loop(0, LON, reply, 0)
+            lax.fori_loop(0, LON, pass_on, 0)
+        pltpu.make_async_copy(relay, relay, relay_send).wait()
+
+    @pl.when(worker)
+    def _():
+        def sent(j, _):
+            pltpu.make_async_copy(back.at[j], back.at[j], ret_send.at[j]).wait()
             return 0
 
-        lax.fori_loop(0, LEV, chunk, 0)
-        pltpu.make_async_copy(back, back, ret_send).wait()
+        lax.fori_loop(0, chunks, sent, 0)
 
     @pl.when(polar)
     def _():
@@ -370,8 +488,9 @@
         ],
         out_specs=[pl.BlockSpec(memory_space=ANY)] * 3,
         scratch_shapes=[
-            VMEM((LEV, LON, NF, TILE, COLS), f32),
-            VMEM((LEV, LON, NF, TILE, COLS), f32),
+            VMEM((NEAR_LEV, LON, NF, TILE, COLS), f32),
+            VMEM((NEAR_LEV, LON, NF, TILE, COLS), f32),
+            VMEM((LEV - NEAR_LEV, LON, NF, TILE, COLS), f32),
             VMEM((WIDE, 2 * WIDE), jnp.bfloat16),
             VMEM((WIDE, 2 * WIDE), jnp.bfloat16),
             VMEM((256, WIDE), jnp.bfloat16),
@@ -381,16 +500,20 @@
             VMEM((3, ROWS, COLS), f32),
             VMEM((ROWS, COLS), jnp.int32),
             VMEM((4, ROWS, WIDE), f32),
+            VMEM((ROWS, 128), f32),
+            VMEM((ROWS, 128), f32),
             VMEM((4, EXT, WIDE), f32),
-            VMEM((4, EXT, 128), f32),
-            VMEM((4, EXT, 128), f32),
+            VMEM((EXT, 128), f32),
+            VMEM((EXT, 128), f32),
             VMEM((4, EXT, WIDE), f32),
             VMEM((2, EXT, WIDE), f32),
             VMEM((3, ROWS, COLS), f32),
             VMEM((2, ROWS, COLS), f32),
             pltpu.SemaphoreType.DMA,
-            pltpu.SemaphoreType.DMA((LEV,)),
+            pltpu.SemaphoreType.DMA((NEAR_LEV,)),
+            pltpu.SemaphoreType.DMA((NEAR_LEV,)),
             pltpu.SemaphoreType.DMA,
+            pltpu.SemaphoreType.DMA((LEV - NEAR_LEV, LON)),
             pltpu.SemaphoreType.DMA,
             pltpu.SemaphoreType.DMA((8,)),
             pltpu.SemaphoreType.DMA((8,)),

time: 96.5 us -> 70.7 us (0.73)
  the two profiles are of different devices: /device:TPU:97 before, /device:TPU:0 now
where the time goes in v2:
time: 70.7 us; the launch traced here: 70.4 us
  Pallas kernels  69.7 us (99%)
    pallas_call x1, Pallas kernels, body(): pl.pallas_call(wave_kernel, out_shape=(sds((NF, LEV, ROWS, COLS), f32), s...  62.6 us
    pallas_call x1, Pallas kernels, body(): pl.pallas_call(final_kernel, out_shape=(sds((2, LEV, ROWS, COLS), f32), s...  7.14 us

profile of v2, /device:TPU:0, one launch (start us, length us, event | category | flops | bytes accessed | tf_op | source)
XLA Modules:
  0.0 70.4 jit_solution(6029726071170143618)
XLA Ops:
  0.6 62.6 %wave.1 = (f32[4,8,64,450]{3,2,1,0:T(8,128)}, f32[3,64,450]{2,1,0:T(8,128)}, f32[2,64,450]{2,1,0:T(8,128)}) custom-call(f32[4,8,64,450]{3,2,1,0:T(8,128)} %fields.3, f32[3,64,450]{2,1,0:T(8,128)} %baro.1, s32[64,450]{1,0:T(8,128)} %land.1, s32[256]{0:T(256)} %cutoff.1, bf16[512,1024]{1,0:T(8,128)(2,1)} %constant.14.clone.wh_hbm, ...), custom_call_target="tpu_custom_call" | custom-call | tf_op jit(solution)/shard_map/wave/pallas_call | solution.py:473
  63.2 7.1 %final.1 = (f32[2,8,64,450]{3,2,1,0:T(8,128)}, f32[2,8,64,450]{3,2,1,0:T(8,128)}, f32[64,450]{1,0:T(8,128)}) custom-call(s32[1]{0:T(128)} %bitcast.polar, f32[8]{0:T(128)} %thick.1, f32[4,8,64,450]{3,2,1,0:T(8,128)} %fields.3, f32[4,8,64,450]{3,2,1,0:T(8,128)} %get-tuple-element.6.filt, f32[3,64,450]{2,1,0:T(8,128)} %get-tuple-element.7.state, ...), custom_call_target="tpu_custom_call" | custom-call | tf_op jit(solution)/shard_map/final/pallas_call | solution.py:532

commit v3 on v2

--- a/solution.py
+++ b/solution.py
@@ -26,8 +26,10 @@
 HALO = 24
 EXT = ROWS + 2 * HALO
 TILE = 8
-NEAR_LEV = 6
-PER_CHUNK = 4
+CHUNKS = 16
+NEAR = 11
+FAR = CHUNKS - NEAR
+PER_CHUNK = 2
 LANE_TILES = ((0, 128), (128, 256), (256, 384), (384, COLS))
 
 
@@ -68,10 +70,12 @@
     return low + high
 
 
-def put_split(high_ref, low_ref, row, lanes, value):
+def put_split(high_ref, low_ref, s, lanes, re, im):
+    value = jnp.concatenate([re, im], axis=0)
     top = value.astype(jnp.bfloat16)
-    high_ref[row : row + 16, lanes[0] : lanes[1]] = top
-    low_ref[row : row + 16, lanes[0] : lanes[1]] = (value - top.astype(jnp.float32)).astype(jnp.bfloat16)
+    rows = slice(s * 16, s * 16 + 16)
+    high_ref[rows, lanes[0] : lanes[1]] = top
+    low_ref[rows, lanes[0] : lanes[1]] = (value - top.astype(jnp.float32)).astype(jnp.bfloat16)
 
 
 def multiply(high_ref, low_ref, wh_ref, wl_ref, out_ref):
@@ -86,11 +90,7 @@
 
 def filter_chunk(j, recv, back, twist, mask, yh, yl, wh, wl, prod):
     for lo, hi in LANE_TILES:
-        z = []
-        for d in range(LON):
-            re = recv[j, d, 0:2, :, lo:hi].reshape(16, hi - lo)
-            im = recv[j, d, 2:4, :, lo:hi].reshape(16, hi - lo)
-            z.append((re, im))
+        z = [(recv[j, d, 0, :, lo:hi], recv[j, d, 1, :, lo:hi]) for d in range(LON)]
         y = butterflies(z, -1)
         for s in range(LON):
             re, im = y[s]
@@ -98,24 +98,22 @@
                 c = twist[0, s : s + 1, lo:hi]
                 n = twist[1, s : s + 1, lo:hi]
                 re, im = re * c + im * n, im * c - re * n
-            put_split(yh, yl, s * 32, (lo, hi), re)
-            put_split(yh, yl, s * 32 + 16, (lo, hi), im)
+            put_split(yh, yl, s, (lo, hi), re, im)
     multiply(yh, yl, wh, wl, prod)
     for lo, hi in LANE_TILES:
         for s in range(LON):
-            a = slice(s * 32, s * 32 + 16)
-            b = slice(s * 32 + 16, s * 32 + 32)
+            a = slice(s * 16, s * 16 + 8)
+            b = slice(s * 16 + 8, s * 16 + 16)
             keep = mask[s, :, lo:hi]
             re = (prod[a, lo:hi] + prod[b, WIDE + lo : WIDE + hi]) * keep
             im = (prod[b, lo:hi] - prod[a, WIDE + lo : WIDE + hi]) * keep
-            put_split(yh, yl, s * 32, (lo, hi), re)
-            put_split(yh, yl, s * 32 + 16, (lo, hi), im)
+            put_split(yh, yl, s, (lo, hi), re, im)
     multiply(yh, yl, wh, wl, prod)
     for lo, hi in LANE_TILES:
         z = []
         for s in range(LON):
-            a = slice(s * 32, s * 32 + 16)
-            b = slice(s * 32 + 16, s * 32 + 32)
+            a = slice(s * 16, s * 16 + 8)
+            b = slice(s * 16 + 8, s * 16 + 16)
             re = prod[a, lo:hi] - prod[b, WIDE + lo : WIDE + hi]
             im = prod[b, lo:hi] + prod[a, WIDE + lo : WIDE + hi]
             if s:
@@ -125,15 +123,15 @@
             z.append((re, im))
         x = butterflies(z, 1)
         for d in range(LON):
-            back[j, d, 0:2, :, lo:hi] = x[d][0].reshape(2, 8, hi - lo)
-            back[j, d, 2:4, :, lo:hi] = x[d][1].reshape(2, 8, hi - lo)
+            back[j, d, 0, :, lo:hi] = x[d][0]
+            back[j, d, 1, :, lo:hi] = x[d][1]
 
 
 def wave_kernel(
     fields, baro, land, cutoff, wh_hbm, wl_hbm, twist,
     filt, state_out, open_out,
     recv, back, relay, wh, wl, yh, yl, prod, mask,
-    own, own_land, src4, edge_r, edge_l, st_c, st_l, st_r, ext, opens, res_state, res_open,
+    own, own_land, src4, edge_r, edge_l, st_c, st_l, st_r, ext, opens,
     fwd_send, fwd_recv, ret_send, ret_recv, relay_recv, relay_send, halo_send, halo_recv, local_sem,
 ):
     lon = lax.axis_index("lon")
@@ -158,10 +156,16 @@
     load_wh = pltpu.make_async_copy(wh_hbm, wh, local_sem.at[2])
     load_wl = pltpu.make_async_copy(wl_hbm, wl, local_sem.at[3])
 
+    keep_own = pltpu.make_async_copy(fields, filt, local_sem.at[4])
+
     @pl.when(worker)
     def _():
         load_wh.start()
         load_wl.start()
+
+    @pl.when(jnp.logical_not(polar))
+    def _():
+        keep_own.start()
 
     sides = [(dx, dy) for dy in (0, 1, -1) for dx in (-1, 0, 1) if (dx, dy) != (0, 0)]
 
@@ -241,10 +245,13 @@
     extra = jnp.where(polar, 2 * LON + 1, jnp.where(near_y, LON, jnp.where(far, 2 * LON, LON + 1)))
     pl.semaphore_wait(barrier, full + extra)
 
-    def send_level(level, slot, lat_index):
+    def rows_of(ref, q, t):
+        return ref.at[:, q // LEV, lax.rem(q, LEV), pl.ds(pl.multiple_of(t * TILE, TILE), TILE), :]
+
+    def send_chunk(q, slot, lat_index):
         def send_one(t, _):
             pltpu.make_async_remote_copy(
-                src_ref=fields.at[:, level, pl.ds(pl.multiple_of(t * TILE, TILE), TILE), :],
+                src_ref=rows_of(fields, q, t),
                 dst_ref=recv.at[slot, lon],
                 send_sem=fwd_send,
                 recv_sem=fwd_recv.at[slot],
@@ -257,7 +264,7 @@
 
     @pl.when(polar)
     def _():
-        send_level(0, 0, y_lat)
+        send_chunk(0, 0, y_lat)
 
     row_src = {1: slice(ROWS - HALO, ROWS), 0: slice(0, ROWS), -1: slice(0, HALO)}
     row_dst = {1: slice(0, HALO), 0: slice(HALO, HALO + ROWS), -1: slice(HALO + ROWS, EXT)}
@@ -278,16 +285,13 @@
 
     @pl.when(polar)
     def _():
-        for level in range(NEAR_LEV, LEV):
-            send_level(level, level - NEAR_LEV, far_lat)
-            step = level - NEAR_LEV
-            send_level(1 + step, 1 + step, y_lat)
-
-        def more(level, _):
-            send_level(level, level, y_lat)
+        def more(k, _):
+            send_chunk(NEAR + k, k, far_lat)
+            send_chunk(2 * k + 1, 2 * k + 1, y_lat)
+            send_chunk(2 * k + 2, 2 * k + 2, y_lat)
             return 0
 
-        lax.fori_loop(1 + LEV - NEAR_LEV, NEAR_LEV, more, 0)
+        lax.fori_loop(0, FAR, more, 0)
 
     for dy, copy in copies:
         when_inside(dy, copy.wait_send)
@@ -330,16 +334,16 @@
         ext[2] = opens[1] * (north - WAVE * (pltpu.roll(surface, EXT - 1, 0) - surface))
         return carry
 
-    chunks = jnp.where(near_y, NEAR_LEV, jnp.where(far, LEV - NEAR_LEV, 0))
+    chunks = jnp.where(near_y, NEAR, jnp.where(far, FAR, 0))
 
     @pl.when(worker)
     def _():
         load_wh.wait()
         load_wl.wait()
         first = (jnp.where(north, 0, 2) + core) * ROWS + lon * TILE
-        sub = lax.rem(lax.broadcasted_iota(jnp.int32, (16, WIDE), 0), TILE)
-        wave = LON * lax.broadcasted_iota(jnp.int32, (16, WIDE), 1)
-        limit = jnp.zeros((16, WIDE), jnp.int32)
+        sub = lax.broadcasted_iota(jnp.int32, (TILE, WIDE), 0)
+        wave = LON * lax.broadcasted_iota(jnp.int32, (TILE, WIDE), 1)
+        limit = jnp.zeros((TILE, WIDE), jnp.int32)
         for i in range(TILE):
             limit = jnp.where(sub == i, cutoff[first + i], limit)
         for s in range(LON):
@@ -358,7 +362,7 @@
                 def reply(d, _):
                     pltpu.make_async_remote_copy(
                         src_ref=back.at[j, d],
-                        dst_ref=filt.at[:, j, pl.ds(pl.multiple_of(lon * TILE, TILE), TILE), :],
+                        dst_ref=rows_of(filt, j, lon),
                         send_sem=ret_send.at[j],
                         recv_sem=ret_recv,
                         device_id={"lon": d, "lat": home},
@@ -394,24 +398,20 @@
     inner = slice(HALO, HALO + ROWS)
     for c in range(3):
         moved = pltpu.roll(ext[c, inner, :], WIDE - HALO, 1)
-        res_state[c] = moved[:, :COLS]
+        state_out[c] = moved[:, :COLS]
     for c in range(2):
         moved = pltpu.roll(opens[c, inner, :], WIDE - HALO, 1)
-        res_open[c] = moved[:, :COLS]
-    save_state = pltpu.make_async_copy(res_state, state_out, local_sem.at[0])
-    save_open = pltpu.make_async_copy(res_open, open_out, local_sem.at[1])
-    save_state.start()
-    save_open.start()
+        open_out[c] = moved[:, :COLS]
 
     @pl.when(relays)
     def _():
-        for j in range(LEV - NEAR_LEV):
-            def pass_on(t, _, j=j):
+        def pass_chunk(j, _):
+            def pass_on(t, _):
                 here = relay.at[j, t]
                 pltpu.make_async_copy(here, here, relay_recv.at[j, t]).wait()
                 pltpu.make_async_remote_copy(
                     src_ref=here,
-                    dst_ref=filt.at[:, NEAR_LEV + j, pl.ds(pl.multiple_of(t * TILE, TILE), TILE), :],
+                    dst_ref=rows_of(filt, NEAR + j, t),
                     send_sem=relay_send,
                     recv_sem=ret_recv,
                     device_id={"lon": lon, "lat": home},
@@ -420,6 +420,9 @@
                 return 0
 
             lax.fori_loop(0, LON, pass_on, 0)
+            return 0
+
+        lax.fori_loop(0, FAR, pass_chunk, 0)
         pltpu.make_async_copy(relay, relay, relay_send).wait()
 
     @pl.when(worker)
@@ -435,68 +438,65 @@
         pltpu.make_async_copy(fields, fields, fwd_send).wait()
         pltpu.make_async_copy(filt, filt, ret_recv).wait()
 
-    save_state.wait()
-    save_open.wait()
-
-
-def final_kernel(polar, thick, fields, filt, state, opens, tracers, velocity, sea):
+    @pl.when(jnp.logical_not(polar))
+    def _():
+        keep_own.wait()
+
+
+def final_kernel(thick, held, state, opens, tracers, velocity, sea):
     total = thick[0]
     for k in range(1, LEV):
         total = total + thick[k]
-    sea[...] = state[0]
-
-    def finish(source):
-        tracers[...] = source[0:2]
-        for c in range(2):
-            column = None
-            for k in range(LEV):
-                term = (thick[k] / total) * source[2 + c, k]
-                column = term if column is None else column + term
-            shift = state[1 + c] - column
-            gate = opens[c]
-            for k in range(LEV):
-                velocity[c, k] = gate * (source[2 + c, k] + shift)
-
-    @pl.when(polar[0] == 1)
-    def _():
-        finish(filt)
-
-    @pl.when(polar[0] == 0)
-    def _():
-        finish(fields)
+    here = pl.ds(pl.multiple_of(pl.program_id(0) * TILE, TILE), TILE)
+    sea[...] = state[0, here, :]
+    for c in range(2):
+        tracers[c] = held[0, c, :, here, :]
+        column = None
+        for k in range(LEV):
+            term = (thick[k] / total) * held[1, c, k, here, :]
+            column = term if column is None else column + term
+        shift = state[1 + c, here, :] - column
+        gate = opens[c, here, :]
+        for k in range(LEV):
+            velocity[c, k] = gate * (held[1, c, k, here, :] + shift)
 
 
 def body(fields, thickness, cutoff, barotropic, land_sea):
     f32 = jnp.float32
     high, low, twist = tables()
     sds = jax.ShapeDtypeStruct
-    filt, state, opens = pl.pallas_call(
+    split = fields.reshape(2, 2, LEV, ROWS, COLS)
+    held, state, opens = pl.pallas_call(
         wave_kernel,
         out_shape=(
-            sds((NF, LEV, ROWS, COLS), f32),
-            sds((3, ROWS, COLS), f32),
-            sds((2, ROWS, COLS), f32),
+            VMEM((2, 2, LEV, ROWS, COLS), f32),
+            VMEM((3, ROWS, COLS), f32),
+            VMEM((2, ROWS, COLS), f32),
         ),
         in_specs=[
-            pl.BlockSpec(memory_space=ANY),
-            pl.BlockSpec(memory_space=ANY),
-            pl.BlockSpec(memory_space=ANY),
+            pl.BlockSpec(memory_space=pltpu.HBM),
+            pl.BlockSpec(memory_space=pltpu.HBM),
+            pl.BlockSpec(memory_space=pltpu.HBM),
             pl.BlockSpec(memory_space=pltpu.SMEM),
-            pl.BlockSpec(memory_space=ANY),
-            pl.BlockSpec(memory_space=ANY),
+            pl.BlockSpec(memory_space=pltpu.HBM),
+            pl.BlockSpec(memory_space=pltpu.HBM),
             pl.BlockSpec(memory_space=VMEM),
         ],
-        out_specs=[pl.BlockSpec(memory_space=ANY)] * 3,
+        out_specs=[
+            pl.BlockSpec(memory_space=VMEM),
+            pl.BlockSpec(memory_space=VMEM),
+            pl.BlockSpec(memory_space=VMEM),
+        ],
         scratch_shapes=[
-            VMEM((NEAR_LEV, LON, NF, TILE, COLS), f32),
-            VMEM((NEAR_LEV, LON, NF, TILE, COLS), f32),
-            VMEM((LEV - NEAR_LEV, LON, NF, TILE, COLS), f32),
+            VMEM((NEAR, LON, 2, TILE, COLS), f32),
+            VMEM((NEAR, LON, 2, TILE, COLS), f32),
+            VMEM((FAR, LON, 2, TILE, COLS), f32),
             VMEM((WIDE, 2 * WIDE), jnp.bfloat16),
             VMEM((WIDE, 2 * WIDE), jnp.bfloat16),
-            VMEM((256, WIDE), jnp.bfloat16),
-            VMEM((256, WIDE), jnp.bfloat16),
-            VMEM((256, 2 * WIDE), f32),
-            VMEM((LON, 16, WIDE), f32),
+            VMEM((128, WIDE), jnp.bfloat16),
+            VMEM((128, WIDE), jnp.bfloat16),
+            VMEM((128, 2 * WIDE), f32),
+            VMEM((LON, TILE, WIDE), f32),
             VMEM((3, ROWS, COLS), f32),
             VMEM((ROWS, COLS), jnp.int32),
             VMEM((4, ROWS, WIDE), f32),
@@ -507,27 +507,22 @@
             VMEM((EXT, 128), f32),
             VMEM((4, EXT, WIDE), f32),
             VMEM((2, EXT, WIDE), f32),
-            VMEM((3, ROWS, COLS), f32),
-            VMEM((2, ROWS, COLS), f32),
             pltpu.SemaphoreType.DMA,
-            pltpu.SemaphoreType.DMA((NEAR_LEV,)),
-            pltpu.SemaphoreType.DMA((NEAR_LEV,)),
+            pltpu.SemaphoreType.DMA((NEAR,)),
+            pltpu.SemaphoreType.DMA((NEAR,)),
             pltpu.SemaphoreType.DMA,
-            pltpu.SemaphoreType.DMA((LEV - NEAR_LEV, LON)),
+            pltpu.SemaphoreType.DMA((FAR, LON)),
             pltpu.SemaphoreType.DMA,
             pltpu.SemaphoreType.DMA((8,)),
             pltpu.SemaphoreType.DMA((8,)),
-            pltpu.SemaphoreType.DMA((4,)),
+            pltpu.SemaphoreType.DMA((5,)),
         ],
         compiler_params=pltpu.CompilerParams(
-            collective_id=0, has_side_effects=True, vmem_limit_bytes=60 * 1024 * 1024
+            collective_id=0, has_side_effects=True, vmem_limit_bytes=58 * 1024 * 1024
         ),
         name="wave",
-    )(fields, barotropic, land_sea, cutoff, jnp.asarray(high), jnp.asarray(low), jnp.asarray(twist))
-
-    lat = lax.axis_index("lat")
-    polar = ((lat < POLE_DEV) | (lat >= LAT - POLE_DEV)).astype(jnp.int32).reshape(1)
-    rows = lambda i, p: (0, i, 0)
+    )(split, barotropic, land_sea, cutoff, jnp.asarray(high), jnp.asarray(low), jnp.asarray(twist))
+
     return tuple(
         pl.pallas_call(
             final_kernel,
@@ -536,24 +531,21 @@
                 sds((2, LEV, ROWS, COLS), f32),
                 sds((ROWS, COLS), f32),
             ),
-            grid_spec=pltpu.PrefetchScalarGridSpec(
-                num_scalar_prefetch=1,
-                grid=(ROWS // TILE,),
-                in_specs=[
-                    pl.BlockSpec(memory_space=pltpu.SMEM),
-                    pl.BlockSpec((NF, LEV, TILE, COLS), lambda i, p: (0, 0, i * (1 - p[0]), 0)),
-                    pl.BlockSpec((NF, LEV, TILE, COLS), lambda i, p: (0, 0, i * p[0], 0)),
-                    pl.BlockSpec((3, TILE, COLS), rows),
-                    pl.BlockSpec((2, TILE, COLS), rows),
-                ],
-                out_specs=[
-                    pl.BlockSpec((2, LEV, TILE, COLS), lambda i, p: (0, 0, i, 0)),
-                    pl.BlockSpec((2, LEV, TILE, COLS), lambda i, p: (0, 0, i, 0)),
-                    pl.BlockSpec((TILE, COLS), lambda i, p: (i, 0)),
-                ],
-            ),
+            grid=(ROWS // TILE,),
+            in_specs=[
+                pl.BlockSpec(memory_space=pltpu.SMEM),
+                pl.BlockSpec(memory_space=VMEM),
+                pl.BlockSpec(memory_space=VMEM),
+                pl.BlockSpec(memory_space=VMEM),
+            ],
+            out_specs=[
+                pl.BlockSpec((2, LEV, TILE, COLS), lambda i: (0, 0, i, 0)),
+                pl.BlockSpec((2, LEV, TILE, COLS), lambda i: (0, 0, i, 0)),
+                pl.BlockSpec((TILE, COLS), lambda i: (i, 0)),
+            ],
+            compiler_params=pltpu.CompilerParams(vmem_limit_bytes=16 * 1024 * 1024),
             name="final",
-        )(polar, thickness, fields, filt, state, opens)
+        )(thickness, held, state, opens)
     )
 
 

time: 70.7 us -> 59.8 us (0.85)
  Pallas kernels: 69.7 us -> 58.9 us
    pallas_call x1, Pallas kernels: 62.6 us -> 54.9 us  [body(): pl.pallas_call(wave_kernel, out_shape=(VMEM((2, 2, LEV, ROWS, COLS), f32)...]
    pallas_call x1, Pallas kernels: 7.14 us -> 4.03 us  [body(): pl.pallas_call(final_kernel, out_shape=(sds((2, LEV, ROWS, COLS), f32), s...]
where the time goes in v3:
time: 59.8 us; the launch traced here: 59.6 us
  Pallas kernels  58.9 us (98%)
  between operations  0.66 us (1%)
    pallas_call x1, Pallas kernels, body(): pl.pallas_call(wave_kernel, out_shape=(VMEM((2, 2, LEV, ROWS, COLS), f32)...  54.9 us
    pallas_call x1, Pallas kernels, body(): pl.pallas_call(final_kernel, out_shape=(sds((2, LEV, ROWS, COLS), f32), s...  4.03 us

profile of v3, /device:TPU:0, one launch (start us, length us, event | category | flops | bytes accessed | tf_op | source)
XLA Modules:
  0.0 59.6 jit_solution(12335928999726984056)
XLA Ops:
  0.6 0.0 copy-start
  0.6 54.9 %wave.1 = (f32[2,2,8,64,450]{4,3,2,1,0:T(8,128)S(1)}, f32[3,64,450]{2,1,0:T(8,128)S(1)}, f32[2,64,450]{2,1,0:T(8,128)S(1)}) custom-call(f32[2,2,8,64,450]{4,3,2,1,0:T(8,128)} %bitcast.1, f32[3,64,450]{2,1,0:T(8,128)} %baro.1, s32[64,450]{1,0:T(8,128)} %land.1, s32[256]{0:T(256)} %cutoff.1, bf16[512,1024]{1,0:T(8,128)(2,1)} %constant.6.clone.wh_hbm, ...), custom_call_target="tpu_custom_call" | custom-call | tf_op jit(solution)/shard_map/wave/pallas_call | solution.py:469
  55.5 0.0 copy-done
  55.5 4.0 %final.1 = (f32[2,8,64,450]{3,2,1,0:T(8,128)}, f32[2,8,64,450]{3,2,1,0:T(8,128)}, f32[64,450]{1,0:T(8,128)}) custom-call(f32[8]{0:T(128)S(1)} %copy-done, f32[2,2,8,64,450]{4,3,2,1,0:T(8,128)S(1)} %get-tuple-element.6.held, f32[3,64,450]{2,1,0:T(8,128)S(1)} %get-tuple-element.7.state, f32[2,64,450]{2,1,0:T(8,128)S(1)} %get-tuple-element.8.opens), custom_call_target="tpu_custom_call" | custom-call | tf_op jit(solution)/shard_map/final/pallas_call | solution.py:527
Async XLA Ops:
  0.6 54.9 %copy-start = (f32[8]{0:T(128)S(1)}, f32[8]{0:T(128)}, u32[]{:S(2)}) copy-start(f32[8]{0:T(128)} %thick.1) | copy-start | bytes 100

commit v4 on v3

--- a/solution.py
+++ b/solution.py
@@ -30,7 +30,10 @@
 NEAR = 11
 FAR = CHUNKS - NEAR
 PER_CHUNK = 2
-LANE_TILES = ((0, 128), (128, 256), (256, 384), (384, COLS))
+MAIN = 384
+PACK = 2 * MAIN + 128
+TAIL = COLS - MAIN
+LANE_TILES = ((0, 128), (128, 256), (256, 384), (384, WIDE))
 
 
 def tables():
@@ -88,9 +91,36 @@
         )
 
 
-def filter_chunk(j, recv, back, twist, mask, yh, yl, wh, wl, prod):
+def lanes_of(rows):
+    return lax.broadcasted_iota(jnp.int32, (rows, 128), 1)
+
+
+def pack_tail(first, second):
+    return jnp.where(lanes_of(first.shape[0]) < 64, first, pltpu.roll(second, 64, 1))
+
+
+def pack_rest(q, first, second, rest):
+    slot = lanes_of(first.shape[0]) // 2
+    rest = jnp.where(slot == 2 * q, pltpu.roll(first, lax.rem(4 * q + 64, 128), 1), rest)
+    return jnp.where(slot == 2 * q + 1, pltpu.roll(second, lax.rem(4 * q + 66, 128), 1), rest)
+
+
+def unpack_tail(q, tail, rest):
+    lane = lanes_of(tail.shape[0])
+    first = jnp.where(lane < 64, tail, pltpu.roll(rest, (192 - 4 * q) % 128, 1))
+    second = jnp.where(lane < 64, pltpu.roll(tail, 64, 1), pltpu.roll(rest, (190 - 4 * q) % 128, 1))
+    return jnp.where(lane < TAIL, first, 0.0), jnp.where(lane < TAIL, second, 0.0)
+
+
+def filter_chunk(j, q, recv, back, twist, mask, yh, yl, wh, wl, prod):
+    got, recv_rest = recv
+    back, back_rest = back
     for lo, hi in LANE_TILES:
-        z = [(recv[j, d, 0, :, lo:hi], recv[j, d, 1, :, lo:hi]) for d in range(LON)]
+        if lo < MAIN:
+            z = [(got[j, d, :, lo:hi], got[j, d, :, MAIN + lo : MAIN + hi]) for d in range(LON)]
+        else:
+            part = jnp.minimum(q, 1)
+            z = [unpack_tail(q, got[j, d, :, 2 * MAIN : PACK], recv_rest[part, d]) for d in range(LON)]
         y = butterflies(z, -1)
         for s in range(LON):
             re, im = y[s]
@@ -123,16 +153,21 @@
             z.append((re, im))
         x = butterflies(z, 1)
         for d in range(LON):
-            back[j, d, 0, :, lo:hi] = x[d][0]
-            back[j, d, 1, :, lo:hi] = x[d][1]
+            if lo < MAIN:
+                back[j, d, :, lo:hi] = x[d][0]
+                back[j, d, :, MAIN + lo : MAIN + hi] = x[d][1]
+            else:
+                back[j, d, :, 2 * MAIN : PACK] = pack_tail(*x[d])
+                back_rest[d] = pack_rest(q, *x[d], back_rest[d])
 
 
 def wave_kernel(
     fields, baro, land, cutoff, wh_hbm, wl_hbm, twist,
-    filt, state_out, open_out,
-    recv, back, relay, wh, wl, yh, yl, prod, mask,
+    held, ret, rest_in, state_out, open_out,
+    recv, recv_rest, back, back_rest, relay, relay_rest, stage, packed, rest_out, wh, wl, yh, yl, prod, mask,
     own, own_land, src4, edge_r, edge_l, st_c, st_l, st_r, ext, opens,
-    fwd_send, fwd_recv, ret_send, ret_recv, relay_recv, relay_send, halo_send, halo_recv, local_sem,
+    fwd_send, fwd_recv, fwd_rest, ret_send, ret_rest, ret_recv,
+    relay_recv, relay_rests, relay_send, halo_send, halo_recv, local_sem, load_sem,
 ):
     lon = lax.axis_index("lon")
     lat = lax.axis_index("lat")
@@ -156,12 +191,26 @@
     load_wh = pltpu.make_async_copy(wh_hbm, wh, local_sem.at[2])
     load_wl = pltpu.make_async_copy(wl_hbm, wl, local_sem.at[3])
 
-    keep_own = pltpu.make_async_copy(fields, filt, local_sem.at[4])
+    keep_own = pltpu.make_async_copy(fields, held, local_sem.at[4])
 
     @pl.when(worker)
     def _():
         load_wh.start()
         load_wl.start()
+
+    def load_chunk(q):
+        at = (q // LEV, lax.rem(q, LEV))
+        return pltpu.make_async_copy(
+            fields.at[:, at[0], at[1]], held.at[:, at[0], at[1]], load_sem.at[q]
+        )
+
+    @pl.when(polar)
+    def _():
+        def start(q, _):
+            load_chunk(q).start()
+            return 0
+
+        lax.fori_loop(0, CHUNKS, start, 0)
 
     @pl.when(jnp.logical_not(polar))
     def _():
@@ -245,25 +294,50 @@
     extra = jnp.where(polar, 2 * LON + 1, jnp.where(near_y, LON, jnp.where(far, 2 * LON, LON + 1)))
     pl.semaphore_wait(barrier, full + extra)
 
-    def rows_of(ref, q, t):
-        return ref.at[:, q // LEV, lax.rem(q, LEV), pl.ds(pl.multiple_of(t * TILE, TILE), TILE), :]
+    def rows(t):
+        return pl.ds(pl.multiple_of(t * TILE, TILE), TILE)
+
+    def push(src, dst, send_sem, recv_sem, lon_index, lat_index):
+        pltpu.make_async_remote_copy(
+            src_ref=src, dst_ref=dst, send_sem=send_sem, recv_sem=recv_sem,
+            device_id={"lon": lon_index, "lat": lat_index}, device_id_type=MESH,
+        ).start()
+
+    def arrived(ref, sem):
+        pltpu.make_async_copy(ref, ref, sem).wait()
+
+    def each_lon(action):
+        def one(t, _):
+            action(t)
+            return 0
+
+        lax.fori_loop(0, LON, one, 0)
+
+    def pack_chunk(q, rest):
+        load_chunk(q).wait()
+        for i in range(2):
+            packed[q, :, :, i * MAIN : (i + 1) * MAIN] = held[
+                i, q // LEV, lax.rem(q, LEV), :, 0:MAIN
+            ].reshape(LON, TILE, MAIN)
+            stage[i, :, 0:TAIL] = held[i, q // LEV, lax.rem(q, LEV), :, MAIN:COLS]
+        packed[q, :, :, 2 * MAIN : PACK] = pack_tail(stage[0], stage[1]).reshape(LON, TILE, 128)
+        return pack_rest(q, stage[0], stage[1], rest)
 
     def send_chunk(q, slot, lat_index):
-        def send_one(t, _):
-            pltpu.make_async_remote_copy(
-                src_ref=rows_of(fields, q, t),
-                dst_ref=recv.at[slot, lon],
-                send_sem=fwd_send,
-                recv_sem=fwd_recv.at[slot],
-                device_id={"lon": t, "lat": lat_index},
-                device_id_type=MESH,
-            ).start()
-            return 0
-
-        lax.fori_loop(0, LON, send_one, 0)
+        each_lon(lambda t: push(
+            packed.at[q, t], recv.at[slot, lon], fwd_send.at[0], fwd_recv.at[slot], t, lat_index
+        ))
+
+    def send_rest(part, lat_index, sem):
+        each_lon(lambda t: push(
+            rest_out.at[part, rows(t), :], recv_rest.at[part, lon], fwd_send.at[sem], fwd_rest.at[part, lon],
+            t, lat_index,
+        ))
 
     @pl.when(polar)
     def _():
+        rest_out[0] = pack_chunk(0, jnp.zeros((ROWS, 128), jnp.float32))
+        send_rest(0, y_lat, 1)
         send_chunk(0, 0, y_lat)
 
     row_src = {1: slice(ROWS - HALO, ROWS), 0: slice(0, ROWS), -1: slice(0, HALO)}
@@ -285,13 +359,21 @@
 
     @pl.when(polar)
     def _():
-        def more(k, _):
+        rest_out[1] = lax.fori_loop(1, CHUNKS, pack_chunk, jnp.zeros((ROWS, 128), jnp.float32))
+        send_rest(1, y_lat, 2)
+        send_rest(1, far_lat, 3)
+
+        def step(k, _):
             send_chunk(NEAR + k, k, far_lat)
             send_chunk(2 * k + 1, 2 * k + 1, y_lat)
             send_chunk(2 * k + 2, 2 * k + 2, y_lat)
             return 0
 
-        lax.fori_loop(0, FAR, more, 0)
+        lax.fori_loop(0, FAR, step, 0)
+
+    @pl.when(jnp.logical_not(polar))
+    def _():
+        keep_own.wait()
 
     for dy, copy in copies:
         when_inside(dy, copy.wait_send)
@@ -350,47 +432,50 @@
             m = wave + s
             folded = jnp.minimum(m, NLON - m)
             mask[s] = jnp.where(folded <= limit, 1.0 / NLON, 0.0)
-        yh[...] = jnp.zeros_like(yh)
-        yl[...] = jnp.zeros_like(yl)
+        back_rest[...] = jnp.zeros_like(back_rest)
+        q_first = jnp.where(near_y, 0, NEAR)
+
+        @pl.when(near_y)
+        def _():
+            each_lon(lambda d: arrived(recv_rest.at[0, d], fwd_rest.at[0, d]))
 
         def chunk(j, _):
-            pltpu.make_async_copy(recv.at[j], recv.at[j], fwd_recv.at[j]).wait()
-            filter_chunk(j, recv, back, twist, mask, yh, yl, wh, wl, prod)
+            arrived(recv.at[j], fwd_recv.at[j])
+
+            @pl.when(j == jnp.where(near_y, 1, 0))
+            def _():
+                each_lon(lambda d: arrived(recv_rest.at[1, d], fwd_rest.at[1, d]))
+
+            filter_chunk(
+                j, q_first + j, (recv, recv_rest), (back, back_rest), twist, mask, yh, yl, wh, wl, prod
+            )
 
             @pl.when(near_y)
             def _():
-                def reply(d, _):
-                    pltpu.make_async_remote_copy(
-                        src_ref=back.at[j, d],
-                        dst_ref=rows_of(filt, j, lon),
-                        send_sem=ret_send.at[j],
-                        recv_sem=ret_recv,
-                        device_id={"lon": d, "lat": home},
-                        device_id_type=MESH,
-                    ).start()
-                    return 0
-
-                lax.fori_loop(0, LON, reply, 0)
+                each_lon(lambda d: push(back.at[j, d], ret.at[j, lon], ret_send.at[j], ret_recv.at[0], d, home))
 
             @pl.when(far)
             def _():
-                def reply(d, _):
-                    pltpu.make_async_remote_copy(
-                        src_ref=back.at[j, d],
-                        dst_ref=relay.at[j, lon],
-                        send_sem=ret_send.at[j],
-                        recv_sem=relay_recv.at[j, lon],
-                        device_id={"lon": d, "lat": relay_lat},
-                        device_id_type=MESH,
-                    ).start()
-                    return 0
-
-                lax.fori_loop(0, LON, reply, 0)
+                each_lon(lambda d: push(
+                    back.at[j, d], relay.at[j, lon], ret_send.at[j], relay_recv.at[j, lon], d, relay_lat
+                ))
 
             lax.fori_loop(0, jnp.where(j < SUB // PER_CHUNK, PER_CHUNK, 0), subcycle, 0)
             return 0
 
         lax.fori_loop(0, chunks, chunk, 0)
+
+        @pl.when(near_y)
+        def _():
+            each_lon(lambda d: push(
+                back_rest.at[d], rest_in.at[0, lon], ret_rest, ret_recv.at[1], d, home
+            ))
+
+        @pl.when(far)
+        def _():
+            each_lon(lambda d: push(
+                back_rest.at[d], relay_rest.at[lon], ret_rest, relay_rests.at[lon], d, relay_lat
+            ))
 
     left_over = SUB - PER_CHUNK * jnp.minimum(chunks, SUB // PER_CHUNK)
     lax.fori_loop(0, left_over, subcycle, 0)
@@ -406,59 +491,83 @@
     @pl.when(relays)
     def _():
         def pass_chunk(j, _):
-            def pass_on(t, _):
-                here = relay.at[j, t]
-                pltpu.make_async_copy(here, here, relay_recv.at[j, t]).wait()
-                pltpu.make_async_remote_copy(
-                    src_ref=here,
-                    dst_ref=rows_of(filt, NEAR + j, t),
-                    send_sem=relay_send,
-                    recv_sem=ret_recv,
-                    device_id={"lon": lon, "lat": home},
-                    device_id_type=MESH,
-                ).start()
-                return 0
-
-            lax.fori_loop(0, LON, pass_on, 0)
+            def pass_on(t):
+                arrived(relay.at[j, t], relay_recv.at[j, t])
+                push(relay.at[j, t], ret.at[NEAR + j, t], relay_send.at[0], ret_recv.at[0], lon, home)
+
+            each_lon(pass_on)
             return 0
 
         lax.fori_loop(0, FAR, pass_chunk, 0)
-        pltpu.make_async_copy(relay, relay, relay_send).wait()
+
+        def pass_rest(t):
+            arrived(relay_rest.at[t], relay_rests.at[t])
+            push(relay_rest.at[t], rest_in.at[1, t], relay_send.at[1], ret_recv.at[2], lon, home)
+
+        each_lon(pass_rest)
+        arrived(relay, relay_send.at[0])
+        arrived(relay_rest, relay_send.at[1])
 
     @pl.when(worker)
     def _():
         def sent(j, _):
-            pltpu.make_async_copy(back.at[j], back.at[j], ret_send.at[j]).wait()
+            arrived(back.at[j], ret_send.at[j])
             return 0
 
         lax.fori_loop(0, chunks, sent, 0)
+        arrived(back_rest, ret_rest)
 
     @pl.when(polar)
     def _():
-        pltpu.make_async_copy(fields, fields, fwd_send).wait()
-        pltpu.make_async_copy(filt, filt, ret_recv).wait()
-
-    @pl.when(jnp.logical_not(polar))
-    def _():
-        keep_own.wait()
-
-
-def final_kernel(thick, held, state, opens, tracers, velocity, sea):
+        arrived(packed, fwd_send.at[0])
+        arrived(rest_out.at[0], fwd_send.at[1])
+        arrived(rest_out.at[1], fwd_send.at[2])
+        arrived(rest_out.at[1], fwd_send.at[3])
+        arrived(ret, ret_recv.at[0])
+        arrived(rest_in.at[0], ret_recv.at[1])
+        arrived(rest_in.at[1], ret_recv.at[2])
+
+
+def final_kernel(polar, thick, held, ret, rest_in, state, opens, tracers, velocity, sea):
     total = thick[0]
     for k in range(1, LEV):
         total = total + thick[k]
-    here = pl.ds(pl.multiple_of(pl.program_id(0) * TILE, TILE), TILE)
+    tile = pl.program_id(0)
+    here = pl.ds(pl.multiple_of(tile * TILE, TILE), TILE)
     sea[...] = state[0, here, :]
-    for c in range(2):
-        tracers[c] = held[0, c, :, here, :]
-        column = None
-        for k in range(LEV):
-            term = (thick[k] / total) * held[1, c, k, here, :]
-            column = term if column is None else column + term
-        shift = state[1 + c, here, :] - column
-        gate = opens[c, here, :]
-        for k in range(LEV):
-            velocity[c, k] = gate * (held[1, c, k, here, :] + shift)
+
+    def finish(lo, hi, load):
+        pairs = [[load(c, k) for k in range(LEV)] for c in range(2)]
+        for c in range(2):
+            column = None
+            for k in range(LEV):
+                tracers[c, k, :, lo:hi] = pairs[c][k][0]
+                term = (thick[k] / total) * pairs[c][k][1]
+                column = term if column is None else column + term
+            shift = state[1 + c, here, lo:hi] - column
+            gate = opens[c, here, lo:hi]
+            for k in range(LEV):
+                velocity[c, k, :, lo:hi] = gate * (pairs[c][k][1] + shift)
+
+    @pl.when(polar[0] == 1)
+    def _():
+        for lo in range(0, MAIN, 128):
+            finish(lo, lo + 128, lambda c, k: (
+                ret[c * LEV + k, tile, :, lo : lo + 128],
+                ret[c * LEV + k, tile, :, MAIN + lo : MAIN + lo + 128],
+            ))
+
+        def tail(c, k):
+            q = c * LEV + k
+            first, second = unpack_tail(q, ret[q, tile, :, 2 * MAIN : PACK], rest_in[int(q >= NEAR), tile])
+            return first[:, :TAIL], second[:, :TAIL]
+
+        finish(MAIN, COLS, tail)
+
+    @pl.when(polar[0] == 0)
+    def _():
+        for lo, hi in ((0, 128), (128, 256), (256, MAIN), (MAIN, COLS)):
+            finish(lo, hi, lambda c, k: (held[0, c, k, here, lo:hi], held[1, c, k, here, lo:hi]))
 
 
 def body(fields, thickness, cutoff, barotropic, land_sea):
@@ -466,10 +575,12 @@
     high, low, twist = tables()
     sds = jax.ShapeDtypeStruct
     split = fields.reshape(2, 2, LEV, ROWS, COLS)
-    held, state, opens = pl.pallas_call(
+    held, ret, rest, state, opens = pl.pallas_call(
         wave_kernel,
         out_shape=(
             VMEM((2, 2, LEV, ROWS, COLS), f32),
+            VMEM((CHUNKS, LON, TILE, PACK), f32),
+            VMEM((2, LON, TILE, 128), f32),
             VMEM((3, ROWS, COLS), f32),
             VMEM((2, ROWS, COLS), f32),
         ),
@@ -482,15 +593,17 @@
             pl.BlockSpec(memory_space=pltpu.HBM),
             pl.BlockSpec(memory_space=VMEM),
         ],
-        out_specs=[
-            pl.BlockSpec(memory_space=VMEM),
-            pl.BlockSpec(memory_space=VMEM),
-            pl.BlockSpec(memory_space=VMEM),
-        ],
+        out_specs=[pl.BlockSpec(memory_space=VMEM)] * 5,
         scratch_shapes=[
-            VMEM((NEAR, LON, 2, TILE, COLS), f32),
-            VMEM((NEAR, LON, 2, TILE, COLS), f32),
-            VMEM((FAR, LON, 2, TILE, COLS), f32),
+            VMEM((NEAR, LON, TILE, PACK), f32),
+            VMEM((2, LON, TILE, 128), f32),
+            VMEM((NEAR, LON, TILE, PACK), f32),
+            VMEM((LON, TILE, 128), f32),
+            VMEM((FAR, LON, TILE, PACK), f32),
+            VMEM((LON, TILE, 128), f32),
+            VMEM((2, ROWS, 128), f32),
+            VMEM((CHUNKS, LON, TILE, PACK), f32),
+            VMEM((2, ROWS, 128), f32),
             VMEM((WIDE, 2 * WIDE), jnp.bfloat16),
             VMEM((WIDE, 2 * WIDE), jnp.bfloat16),
             VMEM((128, WIDE), jnp.bfloat16),
@@ -507,22 +620,28 @@
             VMEM((EXT, 128), f32),
             VMEM((4, EXT, WIDE), f32),
             VMEM((2, EXT, WIDE), f32),
-            pltpu.SemaphoreType.DMA,
+            pltpu.SemaphoreType.DMA((4,)),
             pltpu.SemaphoreType.DMA((NEAR,)),
+            pltpu.SemaphoreType.DMA((2, LON)),
             pltpu.SemaphoreType.DMA((NEAR,)),
             pltpu.SemaphoreType.DMA,
+            pltpu.SemaphoreType.DMA((3,)),
             pltpu.SemaphoreType.DMA((FAR, LON)),
-            pltpu.SemaphoreType.DMA,
+            pltpu.SemaphoreType.DMA((LON,)),
+            pltpu.SemaphoreType.DMA((2,)),
             pltpu.SemaphoreType.DMA((8,)),
             pltpu.SemaphoreType.DMA((8,)),
             pltpu.SemaphoreType.DMA((5,)),
+            pltpu.SemaphoreType.DMA((CHUNKS,)),
         ],
         compiler_params=pltpu.CompilerParams(
-            collective_id=0, has_side_effects=True, vmem_limit_bytes=58 * 1024 * 1024
+            collective_id=0, has_side_effects=True, vmem_limit_bytes=53 * 1024 * 1024
         ),
         name="wave",
     )(split, barotropic, land_sea, cutoff, jnp.asarray(high), jnp.asarray(low), jnp.asarray(twist))
 
+    lat = lax.axis_index("lat")
+    polar = ((lat < POLE_DEV) | (lat >= LAT - POLE_DEV)).astype(jnp.int32).reshape(1)
     return tuple(
         pl.pallas_call(
             final_kernel,
@@ -534,6 +653,9 @@
             grid=(ROWS // TILE,),
             in_specs=[
                 pl.BlockSpec(memory_space=pltpu.SMEM),
+                pl.BlockSpec(memory_space=pltpu.SMEM),
+                pl.BlockSpec(memory_space=VMEM),
+                pl.BlockSpec(memory_space=VMEM),
                 pl.BlockSpec(memory_space=VMEM),
                 pl.BlockSpec(memory_space=VMEM),
                 pl.BlockSpec(memory_space=VMEM),
@@ -545,7 +667,7 @@
             ],
             compiler_params=pltpu.CompilerParams(vmem_limit_bytes=16 * 1024 * 1024),
             name="final",
-        )(thickness, held, state, opens)
+        )(polar, thickness, held, ret, rest, state, opens)
     )
 
 

time: 59.8 us -> 58.1 us (0.972)
  Pallas kernels: 58.9 us -> 57.3 us
    pallas_call x1, Pallas kernels: 54.9 us -> 52.7 us  [body(): pl.pallas_call(wave_kernel, out_shape=(VMEM((2, 2, LEV, ROWS, COLS), f32)...]
where the time goes in v4:
time: 58.1 us; the launch traced here: 57.9 us
  Pallas kernels  57.3 us (99%)
  between operations  0.67 us (1%)
    pallas_call x1, Pallas kernels, body(): pl.pallas_call(wave_kernel, out_shape=(VMEM((2, 2, LEV, ROWS, COLS), f32)...  52.7 us
    pallas_call x1, Pallas kernels, body(): pl.pallas_call(final_kernel, out_shape=(sds((2, LEV, ROWS, COLS), f32), s...  4.57 us

profile of v4, /device:TPU:0, one launch (start us, length us, event | category | flops | bytes accessed | tf_op | source)
XLA Modules:
  0.0 57.9 jit_solution(13957615478046373400)
XLA Ops:
  0.6 0.0 copy-start
  0.7 52.7 %wave.1 = (f32[2,2,8,64,450]{4,3,2,1,0:T(8,128)S(1)}, f32[16,8,8,896]{3,2,1,0:T(8,128)S(1)}, f32[2,8,8,128]{3,2,1,0:T(8,128)S(1)}, f32[3,64,450]{2,1,0:T(8,128)S(1)}, f32[2,64,450]{2,1,0:T(8,128)S(1)}) custom-call(f32[2,2,8,64,450]{4,3,2,1,0:T(8,128)} %bitcast.2, f32[3,64,450]{2,1,0:T(8,128)} %baro.1, s32[64,450]{1,0:T(8,128)} %land.1, s32[256]{0:T(256)} %cutoff.1, ...), custom_call_target="tpu_custom_call" | custom-call | tf_op jit(solution)/shard_map/wave/pallas_call | solution.py:578
  53.4 0.0 copy-done
  53.4 4.6 %final.1 = (f32[2,8,64,450]{3,2,1,0:T(8,128)}, f32[2,8,64,450]{3,2,1,0:T(8,128)}, f32[64,450]{1,0:T(8,128)}) custom-call(s32[1]{0:T(128)} %bitcast.polar, f32[8]{0:T(128)S(1)} %copy-done, f32[2,2,8,64,450]{4,3,2,1,0:T(8,128)S(1)} %get-tuple-element.8.held, f32[16,8,8,896]{3,2,1,0:T(8,128)S(1)} %get-tuple-element.9.ret, ...), custom_call_target="tpu_custom_call" | custom-call | tf_op jit(solution)/shard_map/final/pallas_call | solution.py:646
Async XLA Ops:
  0.6 52.7 %copy-start = (f32[8]{0:T(128)S(1)}, f32[8]{0:T(128)}, u32[]{:S(2)}) copy-start(f32[8]{0:T(128)} %thick.1) | copy-start | bytes 100

commit v5 on v4

--- a/solution.py
+++ b/solution.py
@@ -30,6 +30,7 @@
 NEAR = 11
 FAR = CHUNKS - NEAR
 PER_CHUNK = 2
+FIRST = 2
 MAIN = 384
 PACK = 2 * MAIN + 128
 TAIL = COLS - MAIN
@@ -375,36 +376,37 @@
     def _():
         keep_own.wait()
 
-    for dy, copy in copies:
-        when_inside(dy, copy.wait_send)
-        when_inside(-dy, copy.wait_recv)
-    for dy in (1, -1):
-        @pl.when(jnp.logical_not(inside(-dy)))
-        def _(dy=dy):
-            st_c[:, row_dst[dy], :] = jnp.zeros((4, HALO, WIDE), jnp.float32)
-            st_l[row_dst[dy], :] = jnp.zeros((HALO, 128), jnp.float32)
-            st_r[row_dst[dy], :] = jnp.zeros((HALO, 128), jnp.float32)
-
-    lane_ext = lax.broadcasted_iota(jnp.int32, (EXT, 128), 1)
-    edge = HALO + COLS - 384
-    for c in range(4):
-        mid = pltpu.roll(st_c[c], HALO, 1)
-        ext[c, :, 128:384] = mid[:, 128:384]
-        left = pltpu.roll(st_l[...], 128 - c * HALO, 1) if c else st_l[...]
-        ext[c, :, 0:128] = jnp.where(lane_ext < HALO, left, mid[:, 0:128])
-        right = pltpu.roll(st_r[...], (edge - c * HALO) % 128, 1)
-        right = jnp.where(lane_ext < edge + HALO, right, 0.0)
-        ext[c, :, 384:512] = jnp.where(lane_ext >= edge, right, mid[:, 384:512])
-
-    ocean = ext[3]
-    row_id = lat * ROWS - HALO + lax.broadcasted_iota(jnp.int32, (EXT, WIDE), 0)
-    east_open = ocean * pltpu.roll(ocean, WIDE - 1, 1)
-    north_open = jnp.where(row_id == NLAT - 1, 0.0, ocean * pltpu.roll(ocean, EXT - 1, 0))
-    opens[0] = east_open
-    opens[1] = north_open
-    ext[1] = ext[1] * east_open
-    ext[2] = ext[2] * north_open
-    ext[3] = WAVE * ocean
+    def assemble():
+        for dy, copy in copies:
+            when_inside(dy, copy.wait_send)
+            when_inside(-dy, copy.wait_recv)
+        for dy in (1, -1):
+            @pl.when(jnp.logical_not(inside(-dy)))
+            def _(dy=dy):
+                st_c[:, row_dst[dy], :] = jnp.zeros((4, HALO, WIDE), jnp.float32)
+                st_l[row_dst[dy], :] = jnp.zeros((HALO, 128), jnp.float32)
+                st_r[row_dst[dy], :] = jnp.zeros((HALO, 128), jnp.float32)
+
+        lane_ext = lax.broadcasted_iota(jnp.int32, (EXT, 128), 1)
+        edge = HALO + COLS - 384
+        for c in range(4):
+            mid = pltpu.roll(st_c[c], HALO, 1)
+            ext[c, :, 128:384] = mid[:, 128:384]
+            left = pltpu.roll(st_l[...], 128 - c * HALO, 1) if c else st_l[...]
+            ext[c, :, 0:128] = jnp.where(lane_ext < HALO, left, mid[:, 0:128])
+            right = pltpu.roll(st_r[...], (edge - c * HALO) % 128, 1)
+            right = jnp.where(lane_ext < edge + HALO, right, 0.0)
+            ext[c, :, 384:512] = jnp.where(lane_ext >= edge, right, mid[:, 384:512])
+
+        ocean = ext[3]
+        row_id = lat * ROWS - HALO + lax.broadcasted_iota(jnp.int32, (EXT, WIDE), 0)
+        east_open = ocean * pltpu.roll(ocean, WIDE - 1, 1)
+        north_open = jnp.where(row_id == NLAT - 1, 0.0, ocean * pltpu.roll(ocean, EXT - 1, 0))
+        opens[0] = east_open
+        opens[1] = north_open
+        ext[1] = ext[1] * east_open
+        ext[2] = ext[2] * north_open
+        ext[3] = WAVE * ocean
 
     def subcycle(_, carry):
         east = ext[1]
@@ -417,6 +419,10 @@
         return carry
 
     chunks = jnp.where(near_y, NEAR, jnp.where(far, FAR, 0))
+
+    @pl.when(jnp.logical_not(worker))
+    def _():
+        assemble()
 
     @pl.when(worker)
     def _():
@@ -460,24 +466,25 @@
                     back.at[j, d], relay.at[j, lon], ret_send.at[j], relay_recv.at[j, lon], d, relay_lat
                 ))
 
-            lax.fori_loop(0, jnp.where(j < SUB // PER_CHUNK, PER_CHUNK, 0), subcycle, 0)
+            @pl.when(near_y & (j == NEAR - 1))
+            def _():
+                each_lon(lambda d: push(
+                    back_rest.at[d], rest_in.at[0, lon], ret_rest, ret_recv.at[1], d, home
+                ))
+
+            @pl.when(far & (j == FAR - 1))
+            def _():
+                each_lon(lambda d: push(
+                    back_rest.at[d], relay_rest.at[lon], ret_rest, relay_rests.at[lon], d, relay_lat
+                ))
+
+            pl.when(j == FIRST - 1)(assemble)
+            lax.fori_loop(0, jnp.where(j >= FIRST, PER_CHUNK, 0), subcycle, 0)
             return 0
 
         lax.fori_loop(0, chunks, chunk, 0)
 
-        @pl.when(near_y)
-        def _():
-            each_lon(lambda d: push(
-                back_rest.at[d], rest_in.at[0, lon], ret_rest, ret_recv.at[1], d, home
-            ))
-
-        @pl.when(far)
-        def _():
-            each_lon(lambda d: push(
-                back_rest.at[d], relay_rest.at[lon], ret_rest, relay_rests.at[lon], d, relay_lat
-            ))
-
-    left_over = SUB - PER_CHUNK * jnp.minimum(chunks, SUB // PER_CHUNK)
+    left_over = SUB - PER_CHUNK * jnp.maximum(chunks - FIRST, 0)
     lax.fori_loop(0, left_over, subcycle, 0)
 
     inner = slice(HALO, HALO + ROWS)
@@ -528,46 +535,62 @@
         arrived(rest_in.at[1], ret_recv.at[2])
 
 
-def final_kernel(polar, thick, held, ret, rest_in, state, opens, tracers, velocity, sea):
+def final_kernel(
+    thick, held, ret, rest_in, state, opens, tracers_out, velocity_out, sea_out, tracers, velocity, sems
+):
+    lat = lax.axis_index("lat")
+    polar = (lat < POLE_DEV) | (lat >= LAT - POLE_DEV)
     total = thick[0]
     for k in range(1, LEV):
         total = total + thick[k]
-    tile = pl.program_id(0)
-    here = pl.ds(pl.multiple_of(tile * TILE, TILE), TILE)
-    sea[...] = state[0, here, :]
-
-    def finish(lo, hi, load):
+    save_sea = pltpu.make_async_copy(state.at[0], sea_out, sems.at[2])
+    save_sea.start()
+
+    def finish(tile, lo, hi, load):
+        here = pl.ds(pl.multiple_of(tile * TILE, TILE), TILE)
         pairs = [[load(c, k) for k in range(LEV)] for c in range(2)]
         for c in range(2):
             column = None
             for k in range(LEV):
-                tracers[c, k, :, lo:hi] = pairs[c][k][0]
+                tracers[c, k, here, lo:hi] = pairs[c][k][0]
                 term = (thick[k] / total) * pairs[c][k][1]
                 column = term if column is None else column + term
             shift = state[1 + c, here, lo:hi] - column
             gate = opens[c, here, lo:hi]
             for k in range(LEV):
-                velocity[c, k, :, lo:hi] = gate * (pairs[c][k][1] + shift)
-
-    @pl.when(polar[0] == 1)
-    def _():
-        for lo in range(0, MAIN, 128):
-            finish(lo, lo + 128, lambda c, k: (
-                ret[c * LEV + k, tile, :, lo : lo + 128],
-                ret[c * LEV + k, tile, :, MAIN + lo : MAIN + lo + 128],
-            ))
-
-        def tail(c, k):
-            q = c * LEV + k
-            first, second = unpack_tail(q, ret[q, tile, :, 2 * MAIN : PACK], rest_in[int(q >= NEAR), tile])
-            return first[:, :TAIL], second[:, :TAIL]
-
-        finish(MAIN, COLS, tail)
-
-    @pl.when(polar[0] == 0)
-    def _():
-        for lo, hi in ((0, 128), (128, 256), (256, MAIN), (MAIN, COLS)):
-            finish(lo, hi, lambda c, k: (held[0, c, k, here, lo:hi], held[1, c, k, here, lo:hi]))
+                velocity[c, k, here, lo:hi] = gate * (pairs[c][k][1] + shift)
+
+    def step(tile, _):
+        here = pl.ds(pl.multiple_of(tile * TILE, TILE), TILE)
+
+        @pl.when(polar)
+        def _():
+            for lo in range(0, MAIN, 128):
+                finish(tile, lo, lo + 128, lambda c, k: (
+                    ret[c * LEV + k, tile, :, lo : lo + 128],
+                    ret[c * LEV + k, tile, :, MAIN + lo : MAIN + lo + 128],
+                ))
+
+            def tail(c, k):
+                q = c * LEV + k
+                first, second = unpack_tail(q, ret[q, tile, :, 2 * MAIN : PACK], rest_in[int(q >= NEAR), tile])
+                return first[:, :TAIL], second[:, :TAIL]
+
+            finish(tile, MAIN, COLS, tail)
+
+        @pl.when(jnp.logical_not(polar))
+        def _():
+            for lo, hi in ((0, 128), (128, 256), (256, MAIN), (MAIN, COLS)):
+                finish(tile, lo, hi, lambda c, k: (held[0, c, k, here, lo:hi], held[1, c, k, here, lo:hi]))
+
+        pltpu.make_async_copy(tracers.at[:, :, here, :], tracers_out.at[:, :, here, :], sems.at[0]).start()
+        pltpu.make_async_copy(velocity.at[:, :, here, :], velocity_out.at[:, :, here, :], sems.at[1]).start()
+        return 0
+
+    lax.fori_loop(0, LON, step, 0)
+    pltpu.make_async_copy(tracers, tracers_out, sems.at[0]).wait()
+    pltpu.make_async_copy(velocity, velocity_out, sems.at[1]).wait()
+    save_sea.wait()
 
 
 def body(fields, thickness, cutoff, barotropic, land_sea):
@@ -640,8 +663,6 @@
         name="wave",
     )(split, barotropic, land_sea, cutoff, jnp.asarray(high), jnp.asarray(low), jnp.asarray(twist))
 
-    lat = lax.axis_index("lat")
-    polar = ((lat < POLE_DEV) | (lat >= LAT - POLE_DEV)).astype(jnp.int32).reshape(1)
     return tuple(
         pl.pallas_call(
             final_kernel,
@@ -650,9 +671,7 @@
                 sds((2, LEV, ROWS, COLS), f32),
                 sds((ROWS, COLS), f32),
             ),
-            grid=(ROWS // TILE,),
             in_specs=[
-                pl.BlockSpec(memory_space=pltpu.SMEM),
                 pl.BlockSpec(memory_space=pltpu.SMEM),
                 pl.BlockSpec(memory_space=VMEM),
                 pl.BlockSpec(memory_space=VMEM),
@@ -660,14 +679,15 @@
                 pl.BlockSpec(memory_space=VMEM),
                 pl.BlockSpec(memory_space=VMEM),
             ],
-            out_specs=[
-                pl.BlockSpec((2, LEV, TILE, COLS), lambda i: (0, 0, i, 0)),
-                pl.BlockSpec((2, LEV, TILE, COLS), lambda i: (0, 0, i, 0)),
-                pl.BlockSpec((TILE, COLS), lambda i: (i, 0)),
+            out_specs=[pl.BlockSpec(memory_space=ANY)] * 3,
+            scratch_shapes=[
+                VMEM((2, LEV, ROWS, COLS), f32),
+                VMEM((2, LEV, ROWS, COLS), f32),
+                pltpu.SemaphoreType.DMA((3,)),
             ],
             compiler_params=pltpu.CompilerParams(vmem_limit_bytes=16 * 1024 * 1024),
             name="final",
-        )(polar, thickness, held, ret, rest, state, opens)
+        )(thickness, held, ret, rest, state, opens)
     )
 
 

time: 58.1 us -> 56.3 us (0.969)
  Pallas kernels: 57.3 us -> 55.4 us
    pallas_call x1, Pallas kernels: 4.57 us -> 2.71 us  [body(): pl.pallas_call(final_kernel, out_shape=(sds((2, LEV, ROWS, COLS), f32), s...]
where the time goes in v5:
time: 56.3 us; the launch traced here: 56.1 us
  Pallas kernels  55.4 us (98%)
  between operations  0.66 us (1%)
    pallas_call x1, Pallas kernels, body(): pl.pallas_call(wave_kernel, out_shape=(VMEM((2, 2, LEV, ROWS, COLS), f32)...  52.7 us
    pallas_call x1, Pallas kernels, body(): pl.pallas_call(final_kernel, out_shape=(sds((2, LEV, ROWS, COLS), f32), s...  2.71 us

profile of v5, /device:TPU:0, one launch (start us, length us, event | category | flops | bytes accessed | tf_op | source)
XLA Modules:
  0.0 56.1 jit_solution(11190301408011547676)
XLA Ops:
  0.6 0.0 copy-start
  0.6 52.7 %wave.1 = (f32[2,2,8,64,450]{4,3,2,1,0:T(8,128)S(1)}, f32[16,8,8,896]{3,2,1,0:T(8,128)S(1)}, f32[2,8,8,128]{3,2,1,0:T(8,128)S(1)}, f32[3,64,450]{2,1,0:T(8,128)S(1)}, f32[2,64,450]{2,1,0:T(8,128)S(1)}) custom-call(f32[2,2,8,64,450]{4,3,2,1,0:T(8,128)} %bitcast.1, f32[3,64,450]{2,1,0:T(8,128)} %baro.1, s32[64,450]{1,0:T(8,128)} %land.1, s32[256]{0:T(256)} %cutoff.1, ...), custom_call_target="tpu_custom_call" | custom-call | tf_op jit(solution)/shard_map/wave/pallas_call | solution.py:601
  53.4 0.0 copy-done
  53.4 2.7 %final.1 = (f32[2,8,64,450]{3,2,1,0:T(8,128)}, f32[2,8,64,450]{3,2,1,0:T(8,128)}, f32[64,450]{1,0:T(8,128)}) custom-call(f32[8]{0:T(128)S(1)} %copy-done, f32[2,2,8,64,450]{4,3,2,1,0:T(8,128)S(1)} %get-tuple-element.8.held, f32[16,8,8,896]{3,2,1,0:T(8,128)S(1)} %get-tuple-element.9.ret, f32[2,8,8,128]{3,2,1,0:T(8,128)S(1)} %get-tuple-element.10.rest_in, ...), custom_call_target="tpu_custom_call" | custom-call | tf_op jit(solution)/shard_map/final/pallas_call | solution.py:667
Async XLA Ops:
  0.6 52.7 %copy-start = (f32[8]{0:T(128)S(1)}, f32[8]{0:T(128)}, u32[]{:S(2)}) copy-start(f32[8]{0:T(128)} %thick.1) | copy-start | bytes 100

commit v6 on v5

--- a/solution.py
+++ b/solution.py
@@ -163,8 +163,9 @@
 
 
 def wave_kernel(
-    fields, baro, land, cutoff, wh_hbm, wl_hbm, twist,
-    held, ret, rest_in, state_out, open_out,
+    fields, baro, land, cutoff_hbm, wh_hbm, wl_hbm, twist_hbm, thick_hbm,
+    held, ret, rest_in, state_out, open_out, weights,
+    cutoff, twist, thick,
     recv, recv_rest, back, back_rest, relay, relay_rest, stage, packed, rest_out, wh, wl, yh, yl, prod, mask,
     own, own_land, src4, edge_r, edge_l, st_c, st_l, st_r, ext, opens,
     fwd_send, fwd_recv, fwd_rest, ret_send, ret_rest, ret_recv,
@@ -191,6 +192,10 @@
     load_land.start()
     load_wh = pltpu.make_async_copy(wh_hbm, wh, local_sem.at[2])
     load_wl = pltpu.make_async_copy(wl_hbm, wl, local_sem.at[3])
+    load_twist = pltpu.make_async_copy(twist_hbm, twist, local_sem.at[5])
+    load_cutoff = pltpu.make_async_copy(cutoff_hbm, cutoff, local_sem.at[6])
+    load_thick = pltpu.make_async_copy(thick_hbm, thick, local_sem.at[7])
+    load_thick.start()
 
     keep_own = pltpu.make_async_copy(fields, held, local_sem.at[4])
 
@@ -198,6 +203,8 @@
     def _():
         load_wh.start()
         load_wl.start()
+        load_twist.start()
+        load_cutoff.start()
 
     def load_chunk(q):
         at = (q // LEV, lax.rem(q, LEV))
@@ -428,6 +435,8 @@
     def _():
         load_wh.wait()
         load_wl.wait()
+        load_twist.wait()
+        load_cutoff.wait()
         first = (jnp.where(north, 0, 2) + core) * ROWS + lon * TILE
         sub = lax.broadcasted_iota(jnp.int32, (TILE, WIDE), 0)
         wave = LON * lax.broadcasted_iota(jnp.int32, (TILE, WIDE), 1)
@@ -484,6 +493,13 @@
 
         lax.fori_loop(0, chunks, chunk, 0)
 
+    load_thick.wait()
+    total = thick[0]
+    for k in range(1, LEV):
+        total = total + thick[k]
+    for k in range(LEV):
+        weights[k : k + 1, :] = jnp.full((1, 128), thick[k]) / total
+
     left_over = SUB - PER_CHUNK * jnp.maximum(chunks - FIRST, 0)
     lax.fori_loop(0, left_over, subcycle, 0)
 
@@ -536,13 +552,10 @@
 
 
 def final_kernel(
-    thick, held, ret, rest_in, state, opens, tracers_out, velocity_out, sea_out, tracers, velocity, sems
+    weights, held, ret, rest_in, state, opens, tracers_out, velocity_out, sea_out, tracers, velocity, sems
 ):
     lat = lax.axis_index("lat")
     polar = (lat < POLE_DEV) | (lat >= LAT - POLE_DEV)
-    total = thick[0]
-    for k in range(1, LEV):
-        total = total + thick[k]
     save_sea = pltpu.make_async_copy(state.at[0], sea_out, sems.at[2])
     save_sea.start()
 
@@ -553,7 +566,7 @@
             column = None
             for k in range(LEV):
                 tracers[c, k, here, lo:hi] = pairs[c][k][0]
-                term = (thick[k] / total) * pairs[c][k][1]
+                term = weights[k : k + 1, 0 : hi - lo] * pairs[c][k][1]
                 column = term if column is None else column + term
             shift = state[1 + c, here, lo:hi] - column
             gate = opens[c, here, lo:hi]
@@ -598,7 +611,7 @@
     high, low, twist = tables()
     sds = jax.ShapeDtypeStruct
     split = fields.reshape(2, 2, LEV, ROWS, COLS)
-    held, ret, rest, state, opens = pl.pallas_call(
+    held, ret, rest, state, opens, weights = pl.pallas_call(
         wave_kernel,
         out_shape=(
             VMEM((2, 2, LEV, ROWS, COLS), f32),
@@ -606,18 +619,14 @@
             VMEM((2, LON, TILE, 128), f32),
             VMEM((3, ROWS, COLS), f32),
             VMEM((2, ROWS, COLS), f32),
+            VMEM((LEV, 128), f32),
         ),
-        in_specs=[
-            pl.BlockSpec(memory_space=pltpu.HBM),
-            pl.BlockSpec(memory_space=pltpu.HBM),
-            pl.BlockSpec(memory_space=pltpu.HBM),
-            pl.BlockSpec(memory_space=pltpu.SMEM),
-            pl.BlockSpec(memory_space=pltpu.HBM),
-            pl.BlockSpec(memory_space=pltpu.HBM),
-            pl.BlockSpec(memory_space=VMEM),
-        ],
-        out_specs=[pl.BlockSpec(memory_space=VMEM)] * 5,
+        in_specs=[pl.BlockSpec(memory_space=pltpu.HBM)] * 8,
+        out_specs=[pl.BlockSpec(memory_space=VMEM)] * 6,
         scratch_shapes=[
+            pltpu.SMEM((2 * POLE_DEV * ROWS,), jnp.int32),
+            VMEM((2, LON, WIDE), f32),
+            pltpu.SMEM((LEV,), f32),
             VMEM((NEAR, LON, TILE, PACK), f32),
             VMEM((2, LON, TILE, 128), f32),
             VMEM((NEAR, LON, TILE, PACK), f32),
@@ -654,14 +663,14 @@
             pltpu.SemaphoreType.DMA((2,)),
             pltpu.SemaphoreType.DMA((8,)),
             pltpu.SemaphoreType.DMA((8,)),
-            pltpu.SemaphoreType.DMA((5,)),
+            pltpu.SemaphoreType.DMA((8,)),
             pltpu.SemaphoreType.DMA((CHUNKS,)),
         ],
         compiler_params=pltpu.CompilerParams(
             collective_id=0, has_side_effects=True, vmem_limit_bytes=53 * 1024 * 1024
         ),
         name="wave",
-    )(split, barotropic, land_sea, cutoff, jnp.asarray(high), jnp.asarray(low), jnp.asarray(twist))
+    )(split, barotropic, land_sea, cutoff, jnp.asarray(high), jnp.asarray(low), jnp.asarray(twist), thickness)
 
     return tuple(
         pl.pallas_call(
@@ -672,7 +681,7 @@
                 sds((ROWS, COLS), f32),
             ),
             in_specs=[
-                pl.BlockSpec(memory_space=pltpu.SMEM),
+                pl.BlockSpec(memory_space=VMEM),
                 pl.BlockSpec(memory_space=VMEM),
                 pl.BlockSpec(memory_space=VMEM),
                 pl.BlockSpec(memory_space=VMEM),
@@ -687,7 +696,7 @@
             ],
             compiler_params=pltpu.CompilerParams(vmem_limit_bytes=16 * 1024 * 1024),
             name="final",
-        )(thickness, held, ret, rest, state, opens)
+        )(weights, held, ret, rest, state, opens)
     )
 
 

time: 56.3 us -> 54.9 us (0.975)
  Pallas kernels: 55.4 us -> 54.1 us
    pallas_call x1, Pallas kernels: 52.7 us -> 52 us  [body(): pl.pallas_call(wave_kernel, out_shape=(VMEM((2, 2, LEV, ROWS, COLS), f32)...]
where the time goes in v6:
time: 54.9 us; the launch traced here: 54.8 us
  Pallas kernels  54.1 us (99%)
  between operations  0.64 us (1%)
    pallas_call x1, Pallas kernels, body(): pl.pallas_call(wave_kernel, out_shape=(VMEM((2, 2, LEV, ROWS, COLS), f32)...  52 us
    pallas_call x1, Pallas kernels, body(): pl.pallas_call(final_kernel, out_shape=(sds((2, LEV, ROWS, COLS), f32), s...  2.17 us

profile of v6, /device:TPU:0, one launch (start us, length us, event | category | flops | bytes accessed | tf_op | source)
XLA Modules:
  0.0 54.8 jit_solution(369425230173339631)
XLA Ops:
  0.6 52.0 %wave.1 = (f32[2,2,8,64,450]{4,3,2,1,0:T(8,128)S(1)}, f32[16,8,8,896]{3,2,1,0:T(8,128)S(1)}, f32[2,8,8,128]{3,2,1,0:T(8,128)S(1)}, f32[3,64,450]{2,1,0:T(8,128)S...) custom-call(f32[2,2,8,64,450]{4,3,2,1,0:T(8,128)} %bitcast.1, f32[3,64,450]{2,1,0:T(8,128)} %baro.1, ...), custom_call_target="tpu_custom_call" | custom-call | tf_op jit(solution)/shard_map/wave/pallas_call | solution.py:614
  52.6 2.2 %final.1 = (f32[2,8,64,450]{3,2,1,0:T(8,128)}, f32[2,8,64,450]{3,2,1,0:T(8,128)}, f32[64,450]{1,0:T(8,128)}) custom-call(f32[8,128]{1,0:T(8,128)S(1)} %get-tuple-element.9.weights, f32[2,2,8,64,450]{4,3,2,1,0:T(8,128)S(1)} %get-tuple-element.10.held, f32[16,8,8,896]{3,2,1,0:T(8,128)S(1)} %get-tuple-element.11.ret, ...), custom_call_target="tpu_custom_call" | custom-call | tf_op jit(solution)/shard_map/final/pallas_call | solution.py:676

commit v7 on v6

--- a/solution.py
+++ b/solution.py
@@ -188,8 +188,6 @@
 
     load_state = pltpu.make_async_copy(baro, own, local_sem.at[0])
     load_land = pltpu.make_async_copy(land, own_land, local_sem.at[1])
-    load_state.start()
-    load_land.start()
     load_wh = pltpu.make_async_copy(wh_hbm, wh, local_sem.at[2])
     load_wl = pltpu.make_async_copy(wl_hbm, wl, local_sem.at[3])
     load_twist = pltpu.make_async_copy(twist_hbm, twist, local_sem.at[5])
@@ -214,11 +212,18 @@
 
     @pl.when(polar)
     def _():
+        load_chunk(0).start()
+
+    load_state.start()
+    load_land.start()
+
+    @pl.when(polar)
+    def _():
         def start(q, _):
             load_chunk(q).start()
             return 0
 
-        lax.fori_loop(0, CHUNKS, start, 0)
+        lax.fori_loop(1, CHUNKS, start, 0)
 
     @pl.when(jnp.logical_not(polar))
     def _():
@@ -274,6 +279,59 @@
     def _():
         greet_row(far_lat)
         greet_at(lon, home)
+
+    def rows(t):
+        return pl.ds(pl.multiple_of(t * TILE, TILE), TILE)
+
+    def push(src, dst, send_sem, recv_sem, lon_index, lat_index):
+        pltpu.make_async_remote_copy(
+            src_ref=src, dst_ref=dst, send_sem=send_sem, recv_sem=recv_sem,
+            device_id={"lon": lon_index, "lat": lat_index}, device_id_type=MESH,
+        ).start()
+
+    def arrived(ref, sem):
+        pltpu.make_async_copy(ref, ref, sem).wait()
+
+    def each_lon(action):
+        def one(t, _):
+            action(t)
+            return 0
+
+        lax.fori_loop(0, LON, one, 0)
+
+    def pack_chunk(q, rest):
+        load_chunk(q).wait()
+        for i in range(2):
+            packed[q, :, :, i * MAIN : (i + 1) * MAIN] = held[
+                i, q // LEV, lax.rem(q, LEV), :, 0:MAIN
+            ].reshape(LON, TILE, MAIN)
+            stage[i, :, 0:TAIL] = held[i, q // LEV, lax.rem(q, LEV), :, MAIN:COLS]
+        packed[q, :, :, 2 * MAIN : PACK] = pack_tail(stage[0], stage[1]).reshape(LON, TILE, 128)
+        return pack_rest(q, stage[0], stage[1], rest)
+
+    def send_chunk(q, slot, lat_index):
+        each_lon(lambda t: push(
+            packed.at[q, t], recv.at[slot, lon], fwd_send.at[0], fwd_recv.at[slot], t, lat_index
+        ))
+
+    def send_rest(part, lat_index, sem):
+        each_lon(lambda t: push(
+            rest_out.at[part, rows(t), :], recv_rest.at[part, lon], fwd_send.at[sem], fwd_rest.at[part, lon],
+            t, lat_index,
+        ))
+
+    @pl.when(polar)
+    def _():
+        rest_out[0] = pack_chunk(0, jnp.zeros((ROWS, 128), jnp.float32))
+
+    full = len(sides) - jnp.where((lat == 0) | (lat == LAT - 1), 3, 0)
+    extra = jnp.where(polar, 2 * LON + 1, jnp.where(near_y, LON, jnp.where(far, 2 * LON, LON + 1)))
+    pl.semaphore_wait(barrier, full + extra)
+
+    @pl.when(polar)
+    def _():
+        send_rest(0, y_lat, 1)
+        send_chunk(0, 0, y_lat)
 
     load_state.wait()
     load_land.wait()
@@ -298,56 +356,6 @@
     edge_r[...] = right_pack
     edge_l[...] = left_pack
 
-    full = len(sides) - jnp.where((lat == 0) | (lat == LAT - 1), 3, 0)
-    extra = jnp.where(polar, 2 * LON + 1, jnp.where(near_y, LON, jnp.where(far, 2 * LON, LON + 1)))
-    pl.semaphore_wait(barrier, full + extra)
-
-    def rows(t):
-        return pl.ds(pl.multiple_of(t * TILE, TILE), TILE)
-
-    def push(src, dst, send_sem, recv_sem, lon_index, lat_index):
-        pltpu.make_async_remote_copy(
-            src_ref=src, dst_ref=dst, send_sem=send_sem, recv_sem=recv_sem,
-            device_id={"lon": lon_index, "lat": lat_index}, device_id_type=MESH,
-        ).start()
-
-    def arrived(ref, sem):
-        pltpu.make_async_copy(ref, ref, sem).wait()
-
-    def each_lon(action):
-        def one(t, _):
-            action(t)
-            return 0
-
-        lax.fori_loop(0, LON, one, 0)
-
-    def pack_chunk(q, rest):
-        load_chunk(q).wait()
-        for i in range(2):
-            packed[q, :, :, i * MAIN : (i + 1) * MAIN] = held[
-                i, q // LEV, lax.rem(q, LEV), :, 0:MAIN
-            ].reshape(LON, TILE, MAIN)
-            stage[i, :, 0:TAIL] = held[i, q // LEV, lax.rem(q, LEV), :, MAIN:COLS]
-        packed[q, :, :, 2 * MAIN : PACK] = pack_tail(stage[0], stage[1]).reshape(LON, TILE, 128)
-        return pack_rest(q, stage[0], stage[1], rest)
-
-    def send_chunk(q, slot, lat_index):
-        each_lon(lambda t: push(
-            packed.at[q, t], recv.at[slot, lon], fwd_send.at[0], fwd_recv.at[slot], t, lat_index
-        ))
-
-    def send_rest(part, lat_index, sem):
-        each_lon(lambda t: push(
-            rest_out.at[part, rows(t), :], recv_rest.at[part, lon], fwd_send.at[sem], fwd_rest.at[part, lon],
-            t, lat_index,
-        ))
-
-    @pl.when(polar)
-    def _():
-        rest_out[0] = pack_chunk(0, jnp.zeros((ROWS, 128), jnp.float32))
-        send_rest(0, y_lat, 1)
-        send_chunk(0, 0, y_lat)
-
     row_src = {1: slice(ROWS - HALO, ROWS), 0: slice(0, ROWS), -1: slice(0, HALO)}
     row_dst = {1: slice(0, HALO), 0: slice(HALO, HALO + ROWS), -1: slice(HALO + ROWS, EXT)}
     copies = []
@@ -467,7 +475,13 @@
 
             @pl.when(near_y)
             def _():
-                each_lon(lambda d: push(back.at[j, d], ret.at[j, lon], ret_send.at[j], ret_recv.at[0], d, home))
+                def reply(n):
+                    k = n // 2
+                    hops = jnp.where(k == 0, 2, jnp.where(k == 3, 0, 2 * k - 1))
+                    d = 2 * lax.rem(lon // 2 + hops, LON // 2) + lax.rem(n, 2)
+                    push(back.at[j, d], ret.at[j, lon], ret_send.at[j], ret_recv.at[0], d, home)
+
+                each_lon(reply)
 
             @pl.when(far)
             def _():

time: 54.9 us -> 54.9 us (level)
  no operation moved by 1% of the time
where the time goes in v7:
time: 54.9 us; the launch traced here: 54.8 us
  Pallas kernels  54.1 us (99%)
  between operations  0.64 us (1%)
    pallas_call x1, Pallas kernels, body(): pl.pallas_call(wave_kernel, out_shape=(VMEM((2, 2, LEV, ROWS, COLS), f32)...  52 us
    pallas_call x1, Pallas kernels, body(): pl.pallas_call(final_kernel, out_shape=(sds((2, LEV, ROWS, COLS), f32), s...  2.17 us

profile of v7, /device:TPU:0, one launch (start us, length us, event | category | flops | bytes accessed | tf_op | source)
XLA Modules:
  0.0 54.8 jit_solution(17913120191317914949)
XLA Ops:
  0.6 52.0 %wave.1 = (f32[2,2,8,64,450]{4,3,2,1,0:T(8,128)S(1)}, f32[16,8,8,896]{3,2,1,0:T(8,128)S(1)}, f32[2,8,8,128]{3,2,1,0:T(8,128)S(1)}, f32[3,64,450]{2,1,0:T(8,128)S...) custom-call(f32[2,2,8,64,450]{4,3,2,1,0:T(8,128)} %bitcast.1, f32[3,64,450]{2,1,0:T(8,128)} %baro.1, ...), custom_call_target="tpu_custom_call" | custom-call | tf_op jit(solution)/shard_map/wave/pallas_call | solution.py:628
  52.6 2.2 %final.1 = (f32[2,8,64,450]{3,2,1,0:T(8,128)}, f32[2,8,64,450]{3,2,1,0:T(8,128)}, f32[64,450]{1,0:T(8,128)}) custom-call(f32[8,128]{1,0:T(8,128)S(1)} %get-tuple-element.9.weights, f32[2,2,8,64,450]{4,3,2,1,0:T(8,128)S(1)} %get-tuple-element.10.held, f32[16,8,8,896]{3,2,1,0:T(8,128)S(1)} %get-tuple-element.11.ret, ...), custom_call_target="tpu_custom_call" | custom-call | tf_op jit(solution)/shard_map/final/pallas_call | solution.py:690

commit v8 on v7

--- a/solution.py
+++ b/solution.py
@@ -375,12 +375,15 @@
 
     @pl.when(polar)
     def _():
-        rest_out[1] = lax.fori_loop(1, CHUNKS, pack_chunk, jnp.zeros((ROWS, 128), jnp.float32))
+        rest = pack_chunk(NEAR, jnp.zeros((ROWS, 128), jnp.float32))
+        send_chunk(NEAR, 0, far_lat)
+        rest = lax.fori_loop(1, NEAR, pack_chunk, rest)
+        rest_out[1] = lax.fori_loop(NEAR + 1, CHUNKS, pack_chunk, rest)
         send_rest(1, y_lat, 2)
         send_rest(1, far_lat, 3)
 
         def step(k, _):
-            send_chunk(NEAR + k, k, far_lat)
+            pl.when(k > 0)(lambda: send_chunk(NEAR + k, k, far_lat))
             send_chunk(2 * k + 1, 2 * k + 1, y_lat)
             send_chunk(2 * k + 2, 2 * k + 2, y_lat)
             return 0

time: 54.9 us -> 55.1 us (level)
  no operation moved by 1% of the time
where the time goes in v8:
time: 55.1 us; the launch traced here: 54.8 us
  Pallas kernels  54.1 us (98%)
  between operations  0.64 us (1%)
    pallas_call x1, Pallas kernels, body(): pl.pallas_call(wave_kernel, out_shape=(VMEM((2, 2, LEV, ROWS, COLS), f32)...  52 us
    pallas_call x1, Pallas kernels, body(): pl.pallas_call(final_kernel, out_shape=(sds((2, LEV, ROWS, COLS), f32), s...  2.17 us

profile of v8, /device:TPU:0, one launch (start us, length us, event | category | flops | bytes accessed | tf_op | source)
XLA Modules:
  0.0 54.8 jit_solution(6237319285683105575)
XLA Ops:
  0.6 52.0 %wave.1 = (f32[2,2,8,64,450]{4,3,2,1,0:T(8,128)S(1)}, f32[16,8,8,896]{3,2,1,0:T(8,128)S(1)}, f32[2,8,8,128]{3,2,1,0:T(8,128)S(1)}, f32[3,64,450]{2,1,0:T(8,128)S...) custom-call(f32[2,2,8,64,450]{4,3,2,1,0:T(8,128)} %bitcast.1, f32[3,64,450]{2,1,0:T(8,128)} %baro.1, ...), custom_call_target="tpu_custom_call" | custom-call | tf_op jit(solution)/shard_map/wave/pallas_call | solution.py:631
  52.6 2.2 %final.1 = (f32[2,8,64,450]{3,2,1,0:T(8,128)}, f32[2,8,64,450]{3,2,1,0:T(8,128)}, f32[64,450]{1,0:T(8,128)}) custom-call(f32[8,128]{1,0:T(8,128)S(1)} %get-tuple-element.9.weights, f32[2,2,8,64,450]{4,3,2,1,0:T(8,128)S(1)} %get-tuple-element.10.held, f32[16,8,8,896]{3,2,1,0:T(8,128)S(1)} %get-tuple-element.11.ret, ...), custom_call_target="tpu_custom_call" | custom-call | tf_op jit(solution)/shard_map/final/pallas_call | solution.py:693
